TPU v7x, 512 devices: a whole 4x8x8 slice. The times are simulated.
512 devices in a mesh: ctx: 32 (over y, x), tp: 16 (over z, core).
Axes of the slice: x: 4, y: 8, z: 8, core: 2. Of those that a mesh axis runs over, the one named last changes fastest.
Arguments:
- queries: bfloat16 [8192, 8192], P('ctx', 'tp'), may hold values from -8 to 8
- keys: bfloat16 [8192, 1024], P('ctx'), may hold values from -6 to 6
- values: bfloat16 [8192, 1024], P('ctx'), may hold values from -6 to 6
Outputs:
- attended: bfloat16 [8192, 8192], P('ctx', 'tp')
All inputs are finite; a program needn't handle non-finite values.
Results may differ from a plain program's by a relative error of at most 0.0032.
Values may be sent and summed in bfloat16 or wider, within the bound.
No kernel may reach another device: no remote copies, remote signals or barrier semaphores. Data moves between devices by JAX's collectives and lax.ppermute only.
A program may use at most 64 MiB of HBM per device.

v0:
```python
import functools

import jax
import jax.numpy as jnp
from jax import lax
from jax.experimental import pallas as pl
from jax.experimental.pallas import tpu as pltpu
from jax.sharding import PartitionSpec as P


HEADS = 64
KV_HEADS = 8
HEAD_DIM = 128
GROUP = HEADS // KV_HEADS
Y, X, Z, C = 8, 4, 8, 2
MASKED, EMPTY = -1e30, -1e29
EXPONENT = HEAD_DIM**-0.5 * 1.4426950408889634
TOTAL, PEAK, ROWS = HEAD_DIM, HEAD_DIM + 8, HEAD_DIM + 16


def place(y, x, z, c):
    return (((y % Y) * X + (x % X)) * Z + z) * C + c


def move(a, first, second):
    pairs = [
        (place(y, x, z, c), place(y, x + by, z, c))
        for y in range(Y)
        for x in range(X)
        for z in range(Z)
        for c, by in enumerate((first, second))
    ]
    return lax.ppermute(a, ("ctx", "tp"), pairs)


def swap(a):
    return lax.ppermute(a, "tp", [(i, i ^ 1) for i in range(Z * C)])


def absorb(q_ref, kv_ref, count, delta, head_at, heads, state_in, outs, scores_ref, weights_ref, values_ref):
    rows = q_ref.shape[0]
    half = rows // 2
    values_ref[HEAD_DIM:, :count] = jnp.ones((values_ref.shape[0] - HEAD_DIM, count), jnp.bfloat16)
    for at in range(0, count, rows):
        values_ref[:HEAD_DIM, at : at + rows] = kv_ref[at : at + rows, HEAD_DIM:].T
    ahead = lax.broadcasted_iota(jnp.int32, (half, rows), 0) - lax.broadcasted_iota(jnp.int32, (half, rows), 1)
    per = heads // len(outs)
    first_masked = 0 if count < kv_ref.shape[0] else count // half // 2

    def score(h):
        q = q_ref[:, (head_at + h) * HEAD_DIM : (head_at + h + 1) * HEAD_DIM]
        top = None
        for n in range(count // half):
            at = slice(n * half, (n + 1) * half)
            s = lax.dot_general(
                kv_ref[at, :HEAD_DIM], q, (((1,), (1,)), ((), ())), preferred_element_type=jnp.float32
            )
            if n >= first_masked:
                s = jnp.where(ahead <= -(delta + n * (X * rows)), s, MASKED)
            scores_ref[h % 2, at, :] = s
            t = jnp.max(s.reshape(half // 8, 8, rows), axis=0)
            top = t if top is None else jnp.maximum(top, t)
        return jnp.broadcast_to(jnp.max(top, axis=0, keepdims=True), (8, rows))

    def weigh(h, top):
        old_peak = jnp.full((8, rows), EMPTY, jnp.float32) if state_in is None else state_in[h, PEAK:]
        peak = jnp.maximum(old_peak, top)
        for n in range(count // half):
            at = slice(n * half, (n + 1) * half)
            s = scores_ref[h % 2, at, :].reshape(half // 8, 8, rows)
            w = jnp.exp2((s - peak[None]) * EXPONENT)
            weights_ref[h % 2, at, :] = w.reshape(half, rows).astype(jnp.bfloat16)
        outs[h // per][h % per, PEAK:] = peak
        return None if state_in is None else jnp.exp2((old_peak - peak) * EXPONENT)

    def combine(h, shrink):
        add = jnp.dot(values_ref[:, :count], weights_ref[h % 2, :count, :], preferred_element_type=jnp.float32)[:PEAK]
        if shrink is not None:
            old = state_in[h, :PEAK].reshape(PEAK // 8, 8, rows)
            add = (old * shrink[None]).reshape(PEAK, rows) + add
        outs[h // per][h % per, :PEAK] = add

    top, shrink = {0: score(0)}, {}
    for h in range(heads + 1):
        if h + 1 < heads:
            top[h + 1] = score(h + 1)
        if h >= 1:
            combine(h - 1, shrink[h - 1])
        if h < heads:
            shrink[h] = weigh(h, top[h])


def kernel(head_at, heads, first, n_out, *refs):
    flags, q_ref, kv_ref = refs[:3]
    n = 3
    state_in = None
    if not first:
        state_in = refs[n]
        n += 1
    outs, scratch = refs[n : n + n_out], refs[n + n_out :]
    every = kv_ref.shape[0]

    @pl.when(flags[0] == 0)
    def _():
        for h in range(heads):
            per = heads // n_out
            ref, k = outs[h // per], h % per
            if first:
                ref[k, :PEAK] = jnp.zeros_like(ref[k, :PEAK])
                ref[k, PEAK:] = jnp.full_like(ref[k, PEAK:], EMPTY)
            else:
                ref[k] = state_in[h]

    for n, count in ((1, every // 2), (2, every)):
        pl.when(flags[0] == n)(
            functools.partial(absorb, q_ref, kv_ref, count, flags[1], head_at, heads, state_in, outs, *scratch)
        )


def merge_kernel(mine_ref, theirs_ref, out_ref):
    rows = out_ref.shape[0]
    for h in range(mine_ref.shape[0]):
        peak, peak2 = mine_ref[h, PEAK:], theirs_ref[h, PEAK:]
        top = jnp.maximum(peak, peak2)
        w = jnp.exp2((peak - top) * EXPONENT)
        w2 = jnp.exp2((peak2 - top) * EXPONENT)
        scale = 1.0 / (mine_ref[h, TOTAL:PEAK] * w + theirs_ref[h, TOTAL:PEAK] * w2)
        tiles = (HEAD_DIM // 8, 8, rows)
        normed = mine_ref[h, :HEAD_DIM].reshape(tiles) * (w * scale)[None] + theirs_ref[h, :HEAD_DIM].reshape(
            tiles
        ) * (w2 * scale)[None]
        out_ref[:, h * HEAD_DIM : (h + 1) * HEAD_DIM] = normed.reshape(HEAD_DIM, rows).T.astype(jnp.bfloat16)


VMEM = pl.BlockSpec(memory_space=pltpu.VMEM)
SMEM = pl.BlockSpec(memory_space=pltpu.SMEM)
LIMIT = pltpu.CompilerParams(vmem_limit_bytes=24 * 2**20)


def run(flags, q, kv, state=None, n_out=1, head_at=0):
    rows = q.shape[0]
    heads = GROUP if state is None else state.shape[0]
    keys = kv.shape[0]
    first = state is None
    shape = pltpu.VMEM((heads // n_out, ROWS, rows), jnp.float32)
    return pl.pallas_call(
        functools.partial(kernel, head_at, heads, first, n_out),
        out_shape=shape if n_out == 1 else (shape,) * n_out,
        in_specs=[SMEM] + [VMEM] * (2 + (not first)),
        out_specs=VMEM if n_out == 1 else (VMEM,) * n_out,
        input_output_aliases={} if first or n_out > 1 else {3: 0},
        scratch_shapes=[
            pltpu.VMEM((2, keys, rows), jnp.float32),
            pltpu.VMEM((2, keys, rows), jnp.bfloat16),
            pltpu.VMEM((HEAD_DIM + 16, keys), jnp.bfloat16),
        ],
        cost_estimate=pl.CostEstimate(
            flops=4 * rows * heads * keys * HEAD_DIM,
            bytes_accessed=4 * keys * HEAD_DIM + 2 * rows * heads * HEAD_DIM,
            transcendentals=rows * heads * keys,
        ),
        compiler_params=LIMIT,
    )(flags, q, kv, *(() if first else (state,)))


def spread_kernel(place_ref, keys_ref, values_ref, out_ref):
    both = jnp.concatenate([keys_ref[...], values_ref[...]], 1)
    for n in range(out_ref.shape[0]):
        out_ref[n] = both


def spread(place_of, keys, values, half):
    block = pl.BlockSpec((half, HEAD_DIM), lambda n, at: (at[0], at[1]))
    return pl.pallas_call(
        spread_kernel,
        grid_spec=pltpu.PrefetchScalarGridSpec(
            num_scalar_prefetch=1,
            grid=(1,),
            in_specs=[block, block],
            out_specs=pl.BlockSpec((Y, half, 2 * HEAD_DIM), lambda n, at: (0, 0, 0)),
        ),
        out_shape=jax.ShapeDtypeStruct((Y, half, 2 * HEAD_DIM), jnp.bfloat16),
        compiler_params=LIMIT,
        name="spread",
    )(place_of, *(pltpu.with_memory_space_constraint(a, pltpu.HBM) for a in (keys, values)))


def merge(mine, theirs):
    rows = mine.shape[2]
    return pl.pallas_call(
        merge_kernel,
        out_shape=jax.ShapeDtypeStruct((rows, GROUP // 2 * HEAD_DIM), jnp.bfloat16),
        in_specs=[VMEM] * 2,
        out_specs=VMEM,
        cost_estimate=pl.CostEstimate(flops=rows * HEAD_DIM * 32, bytes_accessed=rows * HEAD_DIM * 32, transcendentals=0),
        compiler_params=LIMIT,
        name="merge",
    )(mine, theirs)


def shards(queries, keys, values):
    ctx, tp = lax.axis_index("ctx"), lax.axis_index("tp")
    y, x, core = ctx // X, ctx % X, tp % C
    rows = queries.shape[0]
    half = rows // 2
    copies = spread(jnp.stack([core, tp // C]).astype(jnp.int32), keys, values, half)
    by_row = lax.all_to_all(
        copies, "ctx", 0, 0, axis_index_groups=[[b * X + a for b in range(Y)] for a in range(X)]
    ).reshape(Y * half, 2 * HEAD_DIM)
    one = move(by_row, 1, -1)
    q = jnp.concatenate([queries, swap(queries)], 1)

    def flags(shift):
        from_x = (x + shift) % X
        delta = (from_x - x - y * X) * rows + core * half
        needed = y + (delta + y * X * rows < rows)
        return jnp.stack([jnp.where(needed == 0, 0, jnp.where(needed <= Y // 2, 1, 2)), delta]).astype(jnp.int32)

    toward = jnp.where(core == 0, -1, 1)
    state = run(flags(0), q, by_row)
    other = move(by_row, -1, 1)
    two = move(one, 1, -1)
    state = run(flags(toward), q, one, state)
    mine, theirs = run(flags(-toward), q, other, state, n_out=2)
    theirs = run(flags(2), q, two, theirs, head_at=GROUP // 2)
    theirs = swap(theirs)
    mine = run(flags(2), q, two, mine)
    return merge(mine, theirs)


def solution(mesh):
    in_specs = (P("ctx", "tp"), P("ctx", None), P("ctx", None))
    return jax.shard_map(shards, mesh=mesh, in_specs=in_specs, out_specs=P("ctx", "tp"), check_vma=False)
```

profile of v0, /device:TPU:1, one launch (start us, length us, event | category | flops | bytes accessed | tf_op | source)
XLA Modules:
  0.0 57.4 jit_solution(2404943272002774353)
XLA Ops:
  0.0 0.1 pad_add_fusion.1.place_ref
  0.1 0.0 copy-start
  0.1 1.4 %spread.1 = bf16[8,128,256]{2,1,0:T(8,128)(2,1)S(1)} custom-call(s32[2]{0:T(128)S(1)} %pad_add_fusion.1.place_ref, bf16[256,1024]{1,0:T(8,128)(2,1)} %keys_ref.1, bf16[256,1024]{1,0:T(8,128)(2,1)} %values_ref.1), custom_call_target="tpu_custom_call" | custom-call | tf_op jit(solution)/shard_map/spread/pallas_call | solution.py:174
  1.4 22.3 %all_to_all.5 = bf16[8,128,256]{2,1,0:T(8,128)(2,1)S(1)} all-to-all(bf16[8,128,256]{2,1,0:T(8,128)(2,1)S(1)} %spread.1), channel_id=1, replica_groups={{0,64,128,192,256,320,384,448},{16,80,144,208,272,336,400,464},{32,96,1..., dimensions={0} | all-to-all | bytes 1048576 | tf_op jit(solution)/shard_map/all_to_all | solution.py:207
  23.8 5.6 %collective-permute-start.1 = (bf16[1024,256]{1,0:T(8,128)(2,1)S(1)}, bf16[1024,256]{1,0:T(8,128)(2,1)S(1)}, u32[]{:S(2)}, u32[]{:S(2)}) collective-permute-start(bf16[1024,256]{1,0:T(8,128)(2,1)S(1)} %bitcast.11), channel_id=1, source_target_pairs={{0,16},{1,49},{2,18},{3,51},{4,20},{5,53},{6,22},{7,55},{8,24},{9,... | collective-permute-start | bytes 1572872 | tf_op jit(solution)/shard_map/ppermute | solution.py:33
  29.4 0.0 copy-done
  29.4 3.3 %collective-permute-start = (bf16[256,512]{1,0:T(8,128)(2,1)S(1)}, bf16[256,512]{1,0:T(8,128)(2,1)S(1)}, u32[]{:S(2)}, u32[]{:S(2)}) collective-permute-start(bf16[256,512]{1,0:T(8,128)(2,1)S(1)} %copy-done), channel_id=1, source_target_pairs={{0,1},{1,0},{2,3},{3,2},{4,5},{5,4},{6,7},{7,6},{8,9},{9,8},{10,11... | collective-permute-start | bytes 786440 | tf_op jit(solution)/shard_map/ppermute | solution.py:37
  32.8 0.1 pad_add_fusion.4.refs_0_
  32.9 0.1 pad_add_fusion.3.refs_0_
  33.0 3.1 %collective-permute-start.3 = (bf16[1024,256]{1,0:T(8,128)(2,1)S(1)}, bf16[1024,256]{1,0:T(8,128)(2,1)S(1)}, u32[]{:S(2)}, u32[]{:S(2)}) collective-permute-start(bf16[1024,256]{1,0:T(8,128)(2,1)S(1)} %bitcast.12), channel_id=1, source_target_pairs={{0,48},{1,17},{2,50},{3,19},{4,52},{5,21},{6,54},{7,23},{8,56},{9,... | collective-permute-start | bytes 1572872 | tf_op jit(solution)/shard_map/ppermute | solution.py:33
  36.1 0.1 pad_add_fusion.2.refs_0_
  36.2 0.0 collective-permute-done.1.refs_2_
  36.2 4.3 %collective-permute-start.2 = (bf16[1024,256]{1,0:T(8,128)(2,1)S(1)}, bf16[1024,256]{1,0:T(8,128)(2,1)S(1)}, u32[]{:S(2)}, u32[]{:S(2)}) collective-permute-start(bf16[1024,256]{1,0:T(8,128)(2,1)S(1)} %collective-permute-done.1.refs_2_), channel_id=1, source_target_pairs={{0,16},{1,49},{2,18},{3,51},{4,20},{5,53},{6,22},{7,55},{8,24},{9,... | collective-permute-start | bytes 1572872 | tf_op jit(solution)/shard_map/ppermute | solution.py:33
  40.5 0.1 pad_add_fusion.refs_0_
  40.6 0.0 collective-permute-done
  40.6 2.4 %shard_map.37.refs_3_ = f32[8,144,256]{2,1,0:T(8,128)S(1)} custom-call(s32[2]{0:T(128)S(1)} %pad_add_fusion.4.refs_0_, bf16[256,1024]{1,0:T(8,128)(2,1)S(1)} %constant_dynamic-update-slice_fusion.refs_1_, bf16[1024,256]{1,0:T(8,128)(2,1)S(1)} %bitcast.13), custom_call_target="tpu_custom_call" | custom-call | flops 1073741824 | bytes 1048576 | tf_op jit(solution)/shard_map/pallas_call | solution.py:146
  43.0 0.7 %shard_map.38.refs_3_ = f32[8,144,256]{2,1,0:T(8,128)S(1)} custom-call(s32[2]{0:T(128)S(1)} %pad_add_fusion.3.refs_0_, bf16[256,1024]{1,0:T(8,128)(2,1)S(1)} %constant_dynamic-update-slice_fusion.refs_1_, bf16[1024,256]{1,0:T(8,128)(2,1)S(1)} %collective-permute-done.1.refs_2_, f32[8,144,256]{2,1,0:T(8,128)S(1)} %shard_map.37.refs_3_), custom_call_target="tpu_custom_call", output_to_operand_aliasing={{}: (3, {})} | custom-call | flops 1073741824 | bytes 1048576 | tf_op jit(solution)/shard_map/pallas_call | solution.py:146
  43.7 0.8 %collective-permute-done.3.refs_2_ = bf16[1024,256]{1,0:T(8,128)(2,1)S(1)} collective-permute-done((bf16[1024,256]{1,0:T(8,128)(2,1)S(1)}, bf16[1024,256]{1,0:T(8,128)(2,1)S(1)}, u32[]{:S(2)}, u32[]{:S(2)}) %collective-permute-start.3) | collective-permute-done | bytes 524320 | tf_op jit(solution)/shard_map/ppermute | solution.py:33
  44.5 0.8 %shard_map.39 = (f32[4,144,256]{2,1,0:T(8,128)S(1)}, f32[4,144,256]{2,1,0:T(8,128)S(1)}) custom-call(s32[2]{0:T(128)S(1)} %pad_add_fusion.2.refs_0_, bf16[256,1024]{1,0:T(8,128)(2,1)S(1)} %constant_dynamic-update-slice_fusion.refs_1_, bf16[1024,256]{1,0:T(8,128)(2,1)S(1)} %collective-permute-done.3.refs_2_, f32[8,144,256]{2,1,0:T(8,128)S(1)} %shard_map.38.refs_3_), custom_call_target="tpu_custom_call" | custom-call | flops 1073741824 | bytes 1048576 | tf_op jit(solution)/shard_map/pallas_call | solution.py:146
  45.3 3.9 %collective-permute-done.2.refs_2_ = bf16[1024,256]{1,0:T(8,128)(2,1)S(1)} collective-permute-done((bf16[1024,256]{1,0:T(8,128)(2,1)S(1)}, bf16[1024,256]{1,0:T(8,128)(2,1)S(1)}, u32[]{:S(2)}, u32[]{:S(2)}) %collective-permute-start.2) | collective-permute-done | bytes 524320 | tf_op jit(solution)/shard_map/ppermute | solution.py:33
  49.3 0.6 %shard_map.41 = f32[4,144,256]{2,1,0:T(8,128)S(1)} custom-call(s32[2]{0:T(128)S(1)} %pad_add_fusion.refs_0_, bf16[256,1024]{1,0:T(8,128)(2,1)S(1)} %constant_dynamic-update-slice_fusion.refs_1_, bf16[1024,256]{1,0:T(8,128)(2,1)S(1)} %collective-permute-done.2.refs_2_, f32[4,144,256]{2,1,0:T(8,128)S(1)} %get-tuple-element.8.refs_3_), custom_call_target="tpu_custom_call", output_to_operand_aliasing={{}: (3, {})} | custom-call | flops 536870912 | bytes 786432 | tf_op jit(solution)/shard_map/pallas_call | solution.py:146
  49.9 5.0 %collective-permute-start.4 = (f32[4,144,256]{2,1,0:T(8,128)S(1)}, f32[4,144,256]{2,1,0:T(8,128)S(1)}, u32[]{:S(2)}, u32[]{:S(2)}) collective-permute-start(f32[4,144,256]{2,1,0:T(8,128)S(1)} %shard_map.41), channel_id=1, source_target_pairs={{0,1},{1,0},{2,3},{3,2},{4,5},{5,4},{6,7},{7,6},{8,9},{9,8},{10,11... | collective-permute-start | bytes 1769480 | tf_op jit(solution)/shard_map/ppermute | solution.py:37
  54.9 0.6 %shard_map.40.mine_ref = f32[4,144,256]{2,1,0:T(8,128)S(1)} custom-call(s32[2]{0:T(128)S(1)} %pad_add_fusion.refs_0_, bf16[256,1024]{1,0:T(8,128)(2,1)S(1)} %constant_dynamic-update-slice_fusion.refs_1_, bf16[1024,256]{1,0:T(8,128)(2,1)S(1)} %collective-permute-done.2.refs_2_, ...), custom_call_target="tpu_custom_call", output_to_operand_aliasing={{}: (3, {})} | custom-call | flops 536870912 | bytes 786432 | tf_op jit(solution)/shard_map/pallas_call | solution.py:146
  55.5 1.0 %collective-permute-done.4.theirs_ref = f32[4,144,256]{2,1,0:T(8,128)S(1)} collective-permute-done((f32[4,144,256]{2,1,0:T(8,128)S(1)}, f32[4,144,256]{2,1,0:T(8,128)S(1)}, u32[]{:S(2)}, u32[]{:S(2)}) %collective-permute-start.4) | collective-permute-done | bytes 589856 | tf_op jit(solution)/shard_map/ppermute | solution.py:37
  56.5 0.9 %merge.1 = bf16[256,512]{1,0:T(8,128)(2,1)} custom-call(f32[4,144,256]{2,1,0:T(8,128)S(1)} %shard_map.40.mine_ref, f32[4,144,256]{2,1,0:T(8,128)S(1)} %collective-permute-done.4.theirs_ref), custom_call_target="tpu_custom_call" | custom-call | flops 1048576 | bytes 1048576 | tf_op jit(solution)/shard_map/merge/pallas_call | solution.py:190
  (2 shorter events, 0.0 us)
Async XLA Ops:
  0.1 29.3 %copy-start = (bf16[256,512]{1,0:T(8,128)(2,1)S(1)}, bf16[256,512]{1,0:T(8,128)(2,1)}, u32[]{:S(2)}) copy-start(bf16[256,512]{1,0:T(8,128)(2,1)} %param.3) | copy-start | bytes 786436
  23.8 12.4 %collective-permute-start.1 = (bf16[1024,256]{1,0:T(8,128)(2,1)S(1)}, bf16[1024,256]{1,0:T(8,128)(2,1)S(1)}, u32[]{:S(2)}, u32[]{:S(2)}) collective-permute-start(bf16[1024,256]{1,0:T(8,128)(2,1)S(1)} %bitcast.11), channel_id=1, source_target_pairs={{0,16},{1,49},{2,18},{3,51},{4,20},{5,53},{6,22},{7,55},{8,24},{9,... | collective-permute-start | bytes 1572872 | tf_op jit(solution)/shard_map/ppermute | solution.py:33
  29.4 11.2 %collective-permute-start = (bf16[256,512]{1,0:T(8,128)(2,1)S(1)}, bf16[256,512]{1,0:T(8,128)(2,1)S(1)}, u32[]{:S(2)}, u32[]{:S(2)}) collective-permute-start(bf16[256,512]{1,0:T(8,128)(2,1)S(1)} %copy-done), channel_id=1, source_target_pairs={{0,1},{1,0},{2,3},{3,2},{4,5},{5,4},{6,7},{7,6},{8,9},{9,8},{10,11... | collective-permute-start | bytes 786440 | tf_op jit(solution)/shard_map/ppermute | solution.py:37
  33.0 11.6 %collective-permute-start.3 = (bf16[1024,256]{1,0:T(8,128)(2,1)S(1)}, bf16[1024,256]{1,0:T(8,128)(2,1)S(1)}, u32[]{:S(2)}, u32[]{:S(2)}) collective-permute-start(bf16[1024,256]{1,0:T(8,128)(2,1)S(1)} %bitcast.12), channel_id=1, source_target_pairs={{0,48},{1,17},{2,50},{3,19},{4,52},{5,21},{6,54},{7,23},{8,56},{9,... | collective-permute-start | bytes 1572872 | tf_op jit(solution)/shard_map/ppermute | solution.py:33
  36.2 13.1 %collective-permute-start.2 = (bf16[1024,256]{1,0:T(8,128)(2,1)S(1)}, bf16[1024,256]{1,0:T(8,128)(2,1)S(1)}, u32[]{:S(2)}, u32[]{:S(2)}) collective-permute-start(bf16[1024,256]{1,0:T(8,128)(2,1)S(1)} %collective-permute-done.1.refs_2_), channel_id=1, source_target_pairs={{0,16},{1,49},{2,18},{3,51},{4,20},{5,53},{6,22},{7,55},{8,24},{9,... | collective-permute-start | bytes 1572872 | tf_op jit(solution)/shard_map/ppermute | solution.py:33
  49.9 6.6 %collective-permute-start.4 = (f32[4,144,256]{2,1,0:T(8,128)S(1)}, f32[4,144,256]{2,1,0:T(8,128)S(1)}, u32[]{:S(2)}, u32[]{:S(2)}) collective-permute-start(f32[4,144,256]{2,1,0:T(8,128)S(1)} %shard_map.41), channel_id=1, source_target_pairs={{0,1},{1,0},{2,3},{3,2},{4,5},{5,4},{6,7},{7,6},{8,9},{9,8},{10,11... | collective-permute-start | bytes 1769480 | tf_op jit(solution)/shard_map/ppermute | solution.py:37
where the time goes:
time: 57.7 us; the launch traced here: 57.4 us
  blocking collectives  22.3 us (39%)
  starting transfers between devices  21.3 us (37%)
  Pallas kernels  7.41 us (13%)
  waiting for transfers between devices  5.71 us (10%)
    all_to_all x1, blocking collectives, shards(): lax.all_to_all(copies, 'ctx', 0, 0, axis_index_groups=[[b * X + a for b i...  22.3 us
    ppermute x3, starting transfers between devices, move(): return lax.ppermute(a, ('ctx', 'tp'), pairs)  13 us
    ppermute x2, starting transfers between devices, swap(): return lax.ppermute(a, 'tp', [(i, i ^ 1) for i in range(Z * C)])  8.21 us
    pallas_call x5, Pallas kernels, run(): pl.pallas_call(functools.partial(kernel, head_at, heads, first, n_out), o...  5.16 us
    ppermute x3, waiting for transfers between devices, move(): return lax.ppermute(a, ('ctx', 'tp'), pairs)  4.75 us
    pallas_call x1, Pallas kernels, spread(): pl.pallas_call(spread_kernel, grid_spec=pltpu.PrefetchScalarGridSpec(num_...  1.35 us
  transfers between devices with their start and end apart: 5, of which 3 were waited for; matrix products, arithmetic and copies ran while one was open for 1% of the time, Pallas kernels for 8%

commit v1 on v0

--- a/solution.py
+++ b/solution.py
@@ -90,9 +90,20 @@
             shrink[h] = weigh(h, top[h])
 
 
-def kernel(head_at, heads, first, n_out, *refs):
-    flags, q_ref, kv_ref = refs[:3]
-    n = 3
+def needs(shift, rows):
+    ctx, core = lax.axis_index("ctx"), lax.rem(lax.axis_index("tp"), C)
+    y, x = lax.div(ctx, X), lax.rem(ctx, X)
+    toward = 2 * core - 1
+    from_x = lax.rem(x + shift * (toward if abs(shift) == 1 else 1) + X, X)
+    delta = (from_x - x - y * X) * rows + core * (rows // 2)
+    needed = y + jnp.where(delta + y * X * rows < rows, 1, 0)
+    return jnp.where(needed == 0, 0, jnp.where(needed <= Y // 2, 1, 2)), delta
+
+
+def kernel(shift, head_at, heads, first, n_out, *refs):
+    q_ref, kv_ref = refs[:2]
+    n = 2
+    amount, delta = needs(shift, q_ref.shape[0])
     state_in = None
     if not first:
         state_in = refs[n]
@@ -100,7 +111,7 @@
     outs, scratch = refs[n : n + n_out], refs[n + n_out :]
     every = kv_ref.shape[0]
 
-    @pl.when(flags[0] == 0)
+    @pl.when(amount == 0)
     def _():
         for h in range(heads):
             per = heads // n_out
@@ -112,8 +123,8 @@
                 ref[k] = state_in[h]
 
     for n, count in ((1, every // 2), (2, every)):
-        pl.when(flags[0] == n)(
-            functools.partial(absorb, q_ref, kv_ref, count, flags[1], head_at, heads, state_in, outs, *scratch)
+        pl.when(amount == n)(
+            functools.partial(absorb, q_ref, kv_ref, count, delta, head_at, heads, state_in, outs, *scratch)
         )
 
 
@@ -133,22 +144,21 @@
 
 
 VMEM = pl.BlockSpec(memory_space=pltpu.VMEM)
-SMEM = pl.BlockSpec(memory_space=pltpu.SMEM)
 LIMIT = pltpu.CompilerParams(vmem_limit_bytes=24 * 2**20)
 
 
-def run(flags, q, kv, state=None, n_out=1, head_at=0):
+def run(shift, q, kv, state=None, n_out=1, head_at=0):
     rows = q.shape[0]
     heads = GROUP if state is None else state.shape[0]
     keys = kv.shape[0]
     first = state is None
     shape = pltpu.VMEM((heads // n_out, ROWS, rows), jnp.float32)
     return pl.pallas_call(
-        functools.partial(kernel, head_at, heads, first, n_out),
+        functools.partial(kernel, shift, head_at, heads, first, n_out),
         out_shape=shape if n_out == 1 else (shape,) * n_out,
-        in_specs=[SMEM] + [VMEM] * (2 + (not first)),
+        in_specs=[VMEM] * (2 + (not first)),
         out_specs=VMEM if n_out == 1 else (VMEM,) * n_out,
-        input_output_aliases={} if first or n_out > 1 else {3: 0},
+        input_output_aliases={} if first or n_out > 1 else {2: 0},
         scratch_shapes=[
             pltpu.VMEM((2, keys, rows), jnp.float32),
             pltpu.VMEM((2, keys, rows), jnp.bfloat16),
@@ -160,29 +170,47 @@
             transcendentals=rows * heads * keys,
         ),
         compiler_params=LIMIT,
-    )(flags, q, kv, *(() if first else (state,)))
-
-
-def spread_kernel(place_ref, keys_ref, values_ref, out_ref):
-    both = jnp.concatenate([keys_ref[...], values_ref[...]], 1)
-    for n in range(out_ref.shape[0]):
-        out_ref[n] = both
-
-
-def spread(place_of, keys, values, half):
-    block = pl.BlockSpec((half, HEAD_DIM), lambda n, at: (at[0], at[1]))
+    )(q, kv, *(() if first else (state,)))
+
+
+def spread_kernel(keys_ref, values_ref, out_ref, block_ref, in_sems, out_sems):
+    half = block_ref.shape[0]
+    tp = lax.axis_index("tp")
+    at = pl.ds(pl.multiple_of(lax.rem(tp, C) * half, half), half)
+    column = pl.ds(pl.multiple_of(lax.div(tp, C) * HEAD_DIM, HEAD_DIM), HEAD_DIM)
+    loads = [
+        pltpu.make_async_copy(
+            ref.at[at, column], block_ref.at[:, n * HEAD_DIM : (n + 1) * HEAD_DIM], in_sems.at[n]
+        )
+        for n, ref in enumerate((keys_ref, values_ref))
+    ]
+    stores = [pltpu.make_async_copy(block_ref, out_ref.at[n], out_sems.at[n]) for n in range(Y)]
+    for copy in loads:
+        copy.start()
+    for copy in loads:
+        copy.wait()
+    for copy in stores:
+        copy.start()
+    for copy in stores:
+        copy.wait()
+
+
+def spread(keys, values):
+    half = keys.shape[0] // C
+    hbm = pl.BlockSpec(memory_space=pltpu.HBM)
     return pl.pallas_call(
         spread_kernel,
-        grid_spec=pltpu.PrefetchScalarGridSpec(
-            num_scalar_prefetch=1,
-            grid=(1,),
-            in_specs=[block, block],
-            out_specs=pl.BlockSpec((Y, half, 2 * HEAD_DIM), lambda n, at: (0, 0, 0)),
-        ),
+        in_specs=[hbm, hbm],
+        out_specs=hbm,
         out_shape=jax.ShapeDtypeStruct((Y, half, 2 * HEAD_DIM), jnp.bfloat16),
+        scratch_shapes=[
+            pltpu.VMEM((half, 2 * HEAD_DIM), jnp.bfloat16),
+            pltpu.SemaphoreType.DMA((2,)),
+            pltpu.SemaphoreType.DMA((Y,)),
+        ],
         compiler_params=LIMIT,
         name="spread",
-    )(place_of, *(pltpu.with_memory_space_constraint(a, pltpu.HBM) for a in (keys, values)))
+    )(keys, values)
 
 
 def merge(mine, theirs):
@@ -199,32 +227,21 @@
 
 
 def shards(queries, keys, values):
-    ctx, tp = lax.axis_index("ctx"), lax.axis_index("tp")
-    y, x, core = ctx // X, ctx % X, tp % C
-    rows = queries.shape[0]
-    half = rows // 2
-    copies = spread(jnp.stack([core, tp // C]).astype(jnp.int32), keys, values, half)
+    half = queries.shape[0] // C
+    copies = spread(keys, values)
     by_row = lax.all_to_all(
         copies, "ctx", 0, 0, axis_index_groups=[[b * X + a for b in range(Y)] for a in range(X)]
     ).reshape(Y * half, 2 * HEAD_DIM)
     one = move(by_row, 1, -1)
     q = jnp.concatenate([queries, swap(queries)], 1)
-
-    def flags(shift):
-        from_x = (x + shift) % X
-        delta = (from_x - x - y * X) * rows + core * half
-        needed = y + (delta + y * X * rows < rows)
-        return jnp.stack([jnp.where(needed == 0, 0, jnp.where(needed <= Y // 2, 1, 2)), delta]).astype(jnp.int32)
-
-    toward = jnp.where(core == 0, -1, 1)
-    state = run(flags(0), q, by_row)
+    state = run(0, q, by_row)
     other = move(by_row, -1, 1)
     two = move(one, 1, -1)
-    state = run(flags(toward), q, one, state)
-    mine, theirs = run(flags(-toward), q, other, state, n_out=2)
-    theirs = run(flags(2), q, two, theirs, head_at=GROUP // 2)
+    state = run(1, q, one, state)
+    mine, theirs = run(-1, q, other, state, n_out=2)
+    theirs = run(2, q, two, theirs, head_at=GROUP // 2)
     theirs = swap(theirs)
-    mine = run(flags(2), q, two, mine)
+    mine = run(2, q, two, mine)
     return merge(mine, theirs)
 
 

time: 57.7 us -> 58.9 us (1.021)
  Pallas kernels: 7.41 us -> 4.14 us
  local copies, waits for them, and re-layouts: 0.05 us -> 2.13 us
  waiting for transfers between devices: 5.71 us -> 7.59 us
  starting transfers between devices: 21.3 us -> 22.2 us
    pallas_call x6, Pallas kernels: 6.51 us -> 3.26 us  [the longest x5 2.46 us: run(): pl.pallas_call(functools.partial(kernel, shift, head_at, heads, first, n_...]
    unnamed x3 -> x7, local copies, waits for them, and re-layouts: 0.03 us -> 2.11 us
    ppermute x3, waiting for transfers between devices: 4.75 us -> 6.09 us  [move(): return lax.ppermute(a, ('ctx', 'tp'), pairs)]
    ppermute x2, starting transfers between devices: 8.21 us -> 8.82 us  [swap(): return lax.ppermute(a, 'tp', [(i, i ^ 1) for i in range(Z * C)])]
  transfers between devices with their start and end apart: 5 -> 5, of which waited for: 3 -> 3; matrix products, arithmetic and copies ran while one was open for 1% -> 0% of each run, Pallas kernels for 8% -> 4%
where the time goes in v1:
time: 58.9 us; the launch traced here: 58.6 us
  blocking collectives  22.3 us (38%)
  starting transfers between devices  22.2 us (38%)
  waiting for transfers between devices  7.59 us (13%)
  Pallas kernels  4.14 us (7%)
  local copies, waits for them, and re-layouts  2.13 us (4%)
    all_to_all x1, blocking collectives, shards(): lax.all_to_all(copies, 'ctx', 0, 0, axis_index_groups=[[b * X + a for b i...  22.3 us
    ppermute x3, starting transfers between devices, move(): return lax.ppermute(a, ('ctx', 'tp'), pairs)  13.4 us
    ppermute x2, starting transfers between devices, swap(): return lax.ppermute(a, 'tp', [(i, i ^ 1) for i in range(Z * C)])  8.82 us
    ppermute x3, waiting for transfers between devices, move(): return lax.ppermute(a, ('ctx', 'tp'), pairs)  6.09 us
    pallas_call x5, Pallas kernels, run(): pl.pallas_call(functools.partial(kernel, shift, head_at, heads, first, n_...  2.46 us
    unnamed x7, local copies, waits for them, and re-layouts  2.11 us
    ppermute x2, waiting for transfers between devices, swap(): return lax.ppermute(a, 'tp', [(i, i ^ 1) for i in range(Z * C)])  1.49 us
  transfers between devices with their start and end apart: 5, of which 3 were waited for; matrix products, arithmetic and copies ran while one was open for 0% of the time, Pallas kernels for 4%

profile of v1, /device:TPU:1, one launch (start us, length us, event | category | flops | bytes accessed | tf_op | source)
XLA Modules:
  0.0 58.6 jit_solution(17508415779373294747)
XLA Ops:
  0.0 0.0 copy-start
  0.0 1.0 %copy-done = bf16[256,1024]{1,0:T(8,128)(2,1)S(1)} copy-done((bf16[256,1024]{1,0:T(8,128)(2,1)S(1)}, bf16[256,1024]{1,0:T(8,128)(2,1)}, u32[]{:S(2)}) %copy-start) | copy-done | bytes 524312
  1.0 0.0 copy-start.1
  1.0 1.0 %copy-done.1 = bf16[256,1024]{1,0:T(8,128)(2,1)S(1)} copy-done((bf16[256,1024]{1,0:T(8,128)(2,1)S(1)}, bf16[256,1024]{1,0:T(8,128)(2,1)}, u32[]{:S(2)}) %copy-start.1) | copy-done | bytes 524312
  2.1 0.0 copy-start.2
  2.1 0.8 %spread.1 = bf16[8,128,256]{2,1,0:T(8,128)(2,1)S(1)} custom-call(bf16[256,1024]{1,0:T(8,128)(2,1)S(1)} %copy-done, bf16[256,1024]{1,0:T(8,128)(2,1)S(1)} %copy-done.1), custom_call_target="tpu_custom_call" | custom-call | tf_op jit(solution)/shard_map/spread/pallas_call | solution.py:201
  2.9 22.3 %all_to_all.5 = bf16[8,128,256]{2,1,0:T(8,128)(2,1)S(1)} all-to-all(bf16[8,128,256]{2,1,0:T(8,128)(2,1)S(1)} %spread.1), channel_id=1, replica_groups={{0,64,128,192,256,320,384,448},{16,80,144,208,272,336,400,464},{32,96,1..., dimensions={0} | all-to-all | bytes 1048576 | tf_op jit(solution)/shard_map/all_to_all | solution.py:232
  25.2 5.6 %collective-permute-start.1 = (bf16[1024,256]{1,0:T(8,128)(2,1)S(1)}, bf16[1024,256]{1,0:T(8,128)(2,1)S(1)}, u32[]{:S(2)}, u32[]{:S(2)}) collective-permute-start(bf16[1024,256]{1,0:T(8,128)(2,1)S(1)} %bitcast.1), channel_id=1, source_target_pairs={{0,16},{1,49},{2,18},{3,51},{4,20},{5,53},{6,22},{7,55},{8,24},{9,... | collective-permute-start | bytes 1572872 | tf_op jit(solution)/shard_map/ppermute | solution.py:33
  30.8 0.0 copy-done.2
  30.8 3.3 %collective-permute-start = (bf16[256,512]{1,0:T(8,128)(2,1)S(1)}, bf16[256,512]{1,0:T(8,128)(2,1)S(1)}, u32[]{:S(2)}, u32[]{:S(2)}) collective-permute-start(bf16[256,512]{1,0:T(8,128)(2,1)S(1)} %copy-done.2), channel_id=1, source_target_pairs={{0,1},{1,0},{2,3},{3,2},{4,5},{5,4},{6,7},{7,6},{8,9},{9,8},{10,11... | collective-permute-start | bytes 786440 | tf_op jit(solution)/shard_map/ppermute | solution.py:37
  34.1 3.1 %collective-permute-start.3 = (bf16[1024,256]{1,0:T(8,128)(2,1)S(1)}, bf16[1024,256]{1,0:T(8,128)(2,1)S(1)}, u32[]{:S(2)}, u32[]{:S(2)}) collective-permute-start(bf16[1024,256]{1,0:T(8,128)(2,1)S(1)} %bitcast.2), channel_id=1, source_target_pairs={{0,48},{1,17},{2,50},{3,19},{4,52},{5,21},{6,54},{7,23},{8,56},{9,... | collective-permute-start | bytes 1572872 | tf_op jit(solution)/shard_map/ppermute | solution.py:33
  37.2 0.0 collective-permute-done.1.refs_1_
  37.2 4.7 %collective-permute-start.2 = (bf16[1024,256]{1,0:T(8,128)(2,1)S(1)}, bf16[1024,256]{1,0:T(8,128)(2,1)S(1)}, u32[]{:S(2)}, u32[]{:S(2)}) collective-permute-start(bf16[1024,256]{1,0:T(8,128)(2,1)S(1)} %collective-permute-done.1.refs_1_), channel_id=1, source_target_pairs={{0,16},{1,49},{2,18},{3,51},{4,20},{5,53},{6,22},{7,55},{8,24},{9,... | collective-permute-start | bytes 1572872 | tf_op jit(solution)/shard_map/ppermute | solution.py:33
  42.0 0.0 collective-permute-done
  42.0 1.8 %shard_map.37.refs_2_ = f32[8,144,256]{2,1,0:T(8,128)S(1)} custom-call(bf16[256,1024]{1,0:T(8,128)(2,1)S(1)} %constant_dynamic-update-slice_fusion.refs_0_, bf16[1024,256]{1,0:T(8,128)(2,1)S(1)} %bitcast.3), custom_call_target="tpu_custom_call" | custom-call | flops 1073741824 | bytes 1048576 | tf_op jit(solution)/shard_map/pallas_call | solution.py:156
  43.9 0.2 shard_map.38.refs_2_
  44.0 1.9 %collective-permute-done.3.refs_1_ = bf16[1024,256]{1,0:T(8,128)(2,1)S(1)} collective-permute-done((bf16[1024,256]{1,0:T(8,128)(2,1)S(1)}, bf16[1024,256]{1,0:T(8,128)(2,1)S(1)}, u32[]{:S(2)}, u32[]{:S(2)}) %collective-permute-start.3) | collective-permute-done | bytes 524320 | tf_op jit(solution)/shard_map/ppermute | solution.py:33
  46.0 0.3 shard_map.39
  46.3 4.2 %collective-permute-done.2.refs_1_ = bf16[1024,256]{1,0:T(8,128)(2,1)S(1)} collective-permute-done((bf16[1024,256]{1,0:T(8,128)(2,1)S(1)}, bf16[1024,256]{1,0:T(8,128)(2,1)S(1)}, u32[]{:S(2)}, u32[]{:S(2)}) %collective-permute-start.2) | collective-permute-done | bytes 524320 | tf_op jit(solution)/shard_map/ppermute | solution.py:33
  50.4 0.1 shard_map.41
  50.5 5.6 %collective-permute-start.4 = (f32[4,144,256]{2,1,0:T(8,128)S(1)}, f32[4,144,256]{2,1,0:T(8,128)S(1)}, u32[]{:S(2)}, u32[]{:S(2)}) collective-permute-start(f32[4,144,256]{2,1,0:T(8,128)S(1)} %shard_map.41), channel_id=1, source_target_pairs={{0,1},{1,0},{2,3},{3,2},{4,5},{5,4},{6,7},{7,6},{8,9},{9,8},{10,11... | collective-permute-start | bytes 1769480 | tf_op jit(solution)/shard_map/ppermute | solution.py:37
  56.1 0.1 shard_map.40.mine_ref
  56.2 1.5 %collective-permute-done.4.theirs_ref = f32[4,144,256]{2,1,0:T(8,128)S(1)} collective-permute-done((f32[4,144,256]{2,1,0:T(8,128)S(1)}, f32[4,144,256]{2,1,0:T(8,128)S(1)}, u32[]{:S(2)}, u32[]{:S(2)}) %collective-permute-start.4) | collective-permute-done | bytes 589856 | tf_op jit(solution)/shard_map/ppermute | solution.py:37
  57.7 0.9 %merge.1 = bf16[256,512]{1,0:T(8,128)(2,1)} custom-call(f32[4,144,256]{2,1,0:T(8,128)S(1)} %shard_map.40.mine_ref, f32[4,144,256]{2,1,0:T(8,128)S(1)} %collective-permute-done.4.theirs_ref), custom_call_target="tpu_custom_call" | custom-call | flops 1048576 | bytes 1048576 | tf_op jit(solution)/shard_map/merge/pallas_call | solution.py:218
  (2 shorter events, 0.0 us)
Async XLA Ops:
  0.0 1.0 %copy-start = (bf16[256,1024]{1,0:T(8,128)(2,1)S(1)}, bf16[256,1024]{1,0:T(8,128)(2,1)}, u32[]{:S(2)}) copy-start(bf16[256,1024]{1,0:T(8,128)(2,1)} %keys_ref.1) | copy-start | bytes 1572868
  1.0 1.0 %copy-start.1 = (bf16[256,1024]{1,0:T(8,128)(2,1)S(1)}, bf16[256,1024]{1,0:T(8,128)(2,1)}, u32[]{:S(2)}) copy-start(bf16[256,1024]{1,0:T(8,128)(2,1)} %values_ref.1) | copy-start | bytes 1572868
  2.1 28.7 %copy-start.2 = (bf16[256,512]{1,0:T(8,128)(2,1)S(1)}, bf16[256,512]{1,0:T(8,128)(2,1)}, u32[]{:S(2)}) copy-start(bf16[256,512]{1,0:T(8,128)(2,1)} %param.3) | copy-start | bytes 786436
  25.2 12.0 %collective-permute-start.1 = (bf16[1024,256]{1,0:T(8,128)(2,1)S(1)}, bf16[1024,256]{1,0:T(8,128)(2,1)S(1)}, u32[]{:S(2)}, u32[]{:S(2)}) collective-permute-start(bf16[1024,256]{1,0:T(8,128)(2,1)S(1)} %bitcast.1), channel_id=1, source_target_pairs={{0,16},{1,49},{2,18},{3,51},{4,20},{5,53},{6,22},{7,55},{8,24},{9,... | collective-permute-start | bytes 1572872 | tf_op jit(solution)/shard_map/ppermute | solution.py:33
  30.8 11.1 %collective-permute-start = (bf16[256,512]{1,0:T(8,128)(2,1)S(1)}, bf16[256,512]{1,0:T(8,128)(2,1)S(1)}, u32[]{:S(2)}, u32[]{:S(2)}) collective-permute-start(bf16[256,512]{1,0:T(8,128)(2,1)S(1)} %copy-done.2), channel_id=1, source_target_pairs={{0,1},{1,0},{2,3},{3,2},{4,5},{5,4},{6,7},{7,6},{8,9},{9,8},{10,11... | collective-permute-start | bytes 786440 | tf_op jit(solution)/shard_map/ppermute | solution.py:37
  34.1 11.9 %collective-permute-start.3 = (bf16[1024,256]{1,0:T(8,128)(2,1)S(1)}, bf16[1024,256]{1,0:T(8,128)(2,1)S(1)}, u32[]{:S(2)}, u32[]{:S(2)}) collective-permute-start(bf16[1024,256]{1,0:T(8,128)(2,1)S(1)} %bitcast.2), channel_id=1, source_target_pairs={{0,48},{1,17},{2,50},{3,19},{4,52},{5,21},{6,54},{7,23},{8,56},{9,... | collective-permute-start | bytes 1572872 | tf_op jit(solution)/shard_map/ppermute | solution.py:33
  37.2 13.2 %collective-permute-start.2 = (bf16[1024,256]{1,0:T(8,128)(2,1)S(1)}, bf16[1024,256]{1,0:T(8,128)(2,1)S(1)}, u32[]{:S(2)}, u32[]{:S(2)}) collective-permute-start(bf16[1024,256]{1,0:T(8,128)(2,1)S(1)} %collective-permute-done.1.refs_1_), channel_id=1, source_target_pairs={{0,16},{1,49},{2,18},{3,51},{4,20},{5,53},{6,22},{7,55},{8,24},{9,... | collective-permute-start | bytes 1572872 | tf_op jit(solution)/shard_map/ppermute | solution.py:33
  50.5 7.2 %collective-permute-start.4 = (f32[4,144,256]{2,1,0:T(8,128)S(1)}, f32[4,144,256]{2,1,0:T(8,128)S(1)}, u32[]{:S(2)}, u32[]{:S(2)}) collective-permute-start(f32[4,144,256]{2,1,0:T(8,128)S(1)} %shard_map.41), channel_id=1, source_target_pairs={{0,1},{1,0},{2,3},{3,2},{4,5},{5,4},{6,7},{7,6},{8,9},{9,8},{10,11... | collective-permute-start | bytes 1769480 | tf_op jit(solution)/shard_map/ppermute | solution.py:37

commit v2 on v1

--- a/solution.py
+++ b/solution.py
@@ -37,44 +37,48 @@
     return lax.ppermute(a, "tp", [(i, i ^ 1) for i in range(Z * C)])
 
 
-def absorb(q_ref, kv_ref, count, delta, head_at, heads, state_in, outs, scores_ref, weights_ref, values_ref):
+def absorb(q_ref, kv_refs, count, delta, masks, head_at, heads, state_in, outs, scores_ref, weights_ref, values_ref):
     rows = q_ref.shape[0]
-    half = rows // 2
-    values_ref[HEAD_DIM:, :count] = jnp.ones((values_ref.shape[0] - HEAD_DIM, count), jnp.bfloat16)
-    for at in range(0, count, rows):
-        values_ref[:HEAD_DIM, at : at + rows] = kv_ref[at : at + rows, HEAD_DIM:].T
-    ahead = lax.broadcasted_iota(jnp.int32, (half, rows), 0) - lax.broadcasted_iota(jnp.int32, (half, rows), 1)
+    sub = rows // C
+    size = kv_refs[0].shape[0]
+    parts = [
+        (kv_refs[at // size], at % size, at // sub * (X * rows), masks[0] <= at < masks[1])
+        for at in range(0, count, sub)
+    ]
+    total = len(parts) * sub
+    values_ref[HEAD_DIM:, :total] = jnp.ones((values_ref.shape[0] - HEAD_DIM, total), jnp.bfloat16)
+    for n, (ref, at, _, _) in enumerate(parts):
+        values_ref[:HEAD_DIM, n * sub : (n + 1) * sub] = ref[at : at + sub, HEAD_DIM:].T
+    ahead = lax.broadcasted_iota(jnp.int32, (sub, rows), 0) - lax.broadcasted_iota(jnp.int32, (sub, rows), 1)
     per = heads // len(outs)
-    first_masked = 0 if count < kv_ref.shape[0] else count // half // 2
 
     def score(h):
         q = q_ref[:, (head_at + h) * HEAD_DIM : (head_at + h + 1) * HEAD_DIM]
         top = None
-        for n in range(count // half):
-            at = slice(n * half, (n + 1) * half)
+        for n, (ref, at, place_of, masked) in enumerate(parts):
             s = lax.dot_general(
-                kv_ref[at, :HEAD_DIM], q, (((1,), (1,)), ((), ())), preferred_element_type=jnp.float32
+                ref[at : at + sub, :HEAD_DIM], q, (((1,), (1,)), ((), ())), preferred_element_type=jnp.float32
             )
-            if n >= first_masked:
-                s = jnp.where(ahead <= -(delta + n * (X * rows)), s, MASKED)
-            scores_ref[h % 2, at, :] = s
-            t = jnp.max(s.reshape(half // 8, 8, rows), axis=0)
+            if masked:
+                s = jnp.where(ahead <= -(delta + place_of), s, MASKED)
+            scores_ref[h % 2, n * sub : (n + 1) * sub, :] = s
+            t = jnp.max(s.reshape(sub // 8, 8, rows), axis=0)
             top = t if top is None else jnp.maximum(top, t)
         return jnp.broadcast_to(jnp.max(top, axis=0, keepdims=True), (8, rows))
 
     def weigh(h, top):
         old_peak = jnp.full((8, rows), EMPTY, jnp.float32) if state_in is None else state_in[h, PEAK:]
         peak = jnp.maximum(old_peak, top)
-        for n in range(count // half):
-            at = slice(n * half, (n + 1) * half)
-            s = scores_ref[h % 2, at, :].reshape(half // 8, 8, rows)
+        for n in range(len(parts)):
+            at = slice(n * sub, (n + 1) * sub)
+            s = scores_ref[h % 2, at, :].reshape(sub // 8, 8, rows)
             w = jnp.exp2((s - peak[None]) * EXPONENT)
-            weights_ref[h % 2, at, :] = w.reshape(half, rows).astype(jnp.bfloat16)
+            weights_ref[h % 2, at, :] = w.reshape(sub, rows).astype(jnp.bfloat16)
         outs[h // per][h % per, PEAK:] = peak
         return None if state_in is None else jnp.exp2((old_peak - peak) * EXPONENT)
 
     def combine(h, shrink):
-        add = jnp.dot(values_ref[:, :count], weights_ref[h % 2, :count, :], preferred_element_type=jnp.float32)[:PEAK]
+        add = jnp.dot(values_ref[:, :total], weights_ref[h % 2, :total, :], preferred_element_type=jnp.float32)[:PEAK]
         if shrink is not None:
             old = state_in[h, :PEAK].reshape(PEAK // 8, 8, rows)
             add = (old * shrink[None]).reshape(PEAK, rows) + add
@@ -100,16 +104,16 @@
     return jnp.where(needed == 0, 0, jnp.where(needed <= Y // 2, 1, 2)), delta
 
 
-def kernel(shift, head_at, heads, first, n_out, *refs):
-    q_ref, kv_ref = refs[:2]
-    n = 2
+def kernel(shift, n_kv, head_at, heads, first, n_out, *refs):
+    q_ref, kv_refs = refs[0], refs[1 : 1 + n_kv]
+    n = 1 + n_kv
     amount, delta = needs(shift, q_ref.shape[0])
+    every = sum(ref.shape[0] for ref in kv_refs)
     state_in = None
     if not first:
         state_in = refs[n]
         n += 1
     outs, scratch = refs[n : n + n_out], refs[n + n_out :]
-    every = kv_ref.shape[0]
 
     @pl.when(amount == 0)
     def _():
@@ -122,9 +126,11 @@
             else:
                 ref[k] = state_in[h]
 
-    for n, count in ((1, every // 2), (2, every)):
+    for n, count, masks in ((1, every // 2, (0, every)), (2, every, (every // 2, every))):
         pl.when(amount == n)(
-            functools.partial(absorb, q_ref, kv_ref, count, delta, head_at, heads, state_in, outs, *scratch)
+            functools.partial(
+                absorb, q_ref, kv_refs, count, delta, masks, head_at, heads, state_in, outs, *scratch
+            )
         )
 
 
@@ -147,18 +153,18 @@
 LIMIT = pltpu.CompilerParams(vmem_limit_bytes=24 * 2**20)
 
 
-def run(shift, q, kv, state=None, n_out=1, head_at=0):
+def run(shift, q, kvs, state=None, n_out=1, head_at=0):
     rows = q.shape[0]
     heads = GROUP if state is None else state.shape[0]
-    keys = kv.shape[0]
+    keys = sum(kv.shape[0] for kv in kvs)
     first = state is None
     shape = pltpu.VMEM((heads // n_out, ROWS, rows), jnp.float32)
     return pl.pallas_call(
-        functools.partial(kernel, shift, head_at, heads, first, n_out),
+        functools.partial(kernel, shift, len(kvs), head_at, heads, first, n_out),
         out_shape=shape if n_out == 1 else (shape,) * n_out,
-        in_specs=[VMEM] * (2 + (not first)),
+        in_specs=[VMEM] * (1 + len(kvs) + (not first)),
         out_specs=VMEM if n_out == 1 else (VMEM,) * n_out,
-        input_output_aliases={} if first or n_out > 1 else {2: 0},
+        input_output_aliases={} if first or n_out > 1 else {1 + len(kvs): 0},
         scratch_shapes=[
             pltpu.VMEM((2, keys, rows), jnp.float32),
             pltpu.VMEM((2, keys, rows), jnp.bfloat16),
@@ -170,7 +176,7 @@
             transcendentals=rows * heads * keys,
         ),
         compiler_params=LIMIT,
-    )(q, kv, *(() if first else (state,)))
+    )(q, *kvs, *(() if first else (state,)))
 
 
 def spread_kernel(keys_ref, values_ref, out_ref, block_ref, in_sems, out_sems):
@@ -210,7 +216,7 @@
         ],
         compiler_params=LIMIT,
         name="spread",
-    )(keys, values)
+    )(*(pltpu.with_memory_space_constraint(a, pltpu.HBM) for a in (keys, values)))
 
 
 def merge(mine, theirs):
@@ -227,21 +233,22 @@
 
 
 def shards(queries, keys, values):
-    half = queries.shape[0] // C
-    copies = spread(keys, values)
-    by_row = lax.all_to_all(
-        copies, "ctx", 0, 0, axis_index_groups=[[b * X + a for b in range(Y)] for a in range(X)]
-    ).reshape(Y * half, 2 * HEAD_DIM)
-    one = move(by_row, 1, -1)
+    groups = [[b * X + a for b in range(Y)] for a in range(X)]
+    own = lax.all_to_all(spread(keys, values), "ctx", 0, 0, axis_index_groups=groups).reshape(-1, 2 * HEAD_DIM)
     q = jnp.concatenate([queries, swap(queries)], 1)
-    state = run(0, q, by_row)
-    other = move(by_row, -1, 1)
-    two = move(one, 1, -1)
-    state = run(1, q, one, state)
-    mine, theirs = run(-1, q, other, state, n_out=2)
-    theirs = run(2, q, two, theirs, head_at=GROUP // 2)
+    near = []
+    for rows in jnp.split(own, 2):
+        near.append(move(rows, 1, -1))
+    other = move(own, -1, 1)
+    far = []
+    for chunk in near:
+        far.append(move(chunk, 1, -1))
+    state = run(0, q, [own])
+    state = run(1, q, near, state)
+    mine, theirs = run(-1, q, [other], state, n_out=2)
+    theirs = run(2, q, far, theirs, head_at=GROUP // 2)
     theirs = swap(theirs)
-    mine = run(2, q, two, mine)
+    mine = run(2, q, far, mine)
     return merge(mine, theirs)
 
 

time: 58.9 us -> 60.7 us (1.031)
  the two profiles are of different devices: /device:TPU:1 before, /device:TPU:241 now
where the time goes in v2:
time: 60.7 us; the launch traced here: 60.4 us
  starting transfers between devices  30.4 us (50%)
  Pallas kernels  15.3 us (25%)
  waiting for transfers between devices  14.5 us (24%)
    ppermute x5, starting transfers between devices, move(): return lax.ppermute(a, ('ctx', 'tp'), pairs)  18.9 us
    pallas_call x5, Pallas kernels, run(): pl.pallas_call(functools.partial(kernel, shift, len(kvs), head_at, heads,...  12.7 us
    all_to_all x1, waiting for transfers between devices, shards(): lax.all_to_all(spread(keys, values), 'ctx', 0, 0, axis_index_groups=groups)  10.7 us
    all_to_all x1, starting transfers between devices, shards(): lax.all_to_all(spread(keys, values), 'ctx', 0, 0, axis_index_groups=groups)  6.43 us
    ppermute x2, starting transfers between devices, swap(): return lax.ppermute(a, 'tp', [(i, i ^ 1) for i in range(Z * C)])  5.05 us
    ppermute x5, waiting for transfers between devices, move(): return lax.ppermute(a, ('ctx', 'tp'), pairs)  3.59 us
    pallas_call x1, Pallas kernels, spread(): pl.pallas_call(spread_kernel, in_specs=[hbm, hbm], out_specs=hbm, out_sha...  1.69 us
  transfers between devices with their start and end apart: 8, of which 3 were waited for; matrix products, arithmetic and copies ran while one was open for 0% of the time, Pallas kernels for 18%

profile of v2, /device:TPU:241, one launch (start us, length us, event | category | flops | bytes accessed | tf_op | source)
XLA Modules:
  0.0 60.4 jit_solution(2889832973247612532)
XLA Ops:
  0.0 0.0 copy-start
  0.0 1.7 %spread.1 = bf16[8,128,256]{2,1,0:T(8,128)(2,1)} custom-call(bf16[256,1024]{1,0:T(8,128)(2,1)} %keys_ref.1, bf16[256,1024]{1,0:T(8,128)(2,1)} %values_ref.1), custom_call_target="tpu_custom_call" | custom-call | tf_op jit(solution)/shard_map/spread/pallas_call | solution.py:207
  1.7 6.4 %all-to-all-start = ((bf16[8,128,256]{2,1,0:T(8,128)(2,1)}), bf16[8,128,256]{2,1,0:T(8,128)(2,1)S(1)}, u32[]{:S(2)}, u32[]{:S(2)}) async-start(bf16[8,128,256]{2,1,0:T(8,128)(2,1)} %spread.1), calls=%async_computation | async-start | bytes 1048576 | tf_op jit(solution)/shard_map/all_to_all | solution.py:237
  8.1 0.0 copy-done
  8.1 3.1 %collective-permute-start = (bf16[256,512]{1,0:T(8,128)(2,1)S(1)}, bf16[256,512]{1,0:T(8,128)(2,1)S(1)}, u32[]{:S(2)}, u32[]{:S(2)}) collective-permute-start(bf16[256,512]{1,0:T(8,128)(2,1)S(1)} %copy-done), channel_id=1, source_target_pairs={{0,1},{1,0},{2,3},{3,2},{4,5},{5,4},{6,7},{7,6},{8,9},{9,8},{10,11... | collective-permute-start | bytes 786440 | tf_op jit(solution)/shard_map/ppermute | solution.py:37
  11.3 10.7 %all-to-all-done = bf16[8,128,256]{2,1,0:T(8,128)(2,1)S(1)} async-done(((bf16[8,128,256]{2,1,0:T(8,128)(2,1)}), bf16[8,128,256]{2,1,0:T(8,128)(2,1)S(1)}, u32[]{:S(2)}, u32[]{:S(2)}) %all-to-all-start) | async-done | bytes 524320 | tf_op jit(solution)/shard_map/all_to_all | solution.py:237
  22.0 3.1 %collective-permute-start.5 = (bf16[1024,256]{1,0:T(8,128)(2,1)S(1)}, bf16[1024,256]{1,0:T(8,128)(2,1)S(1)}, u32[]{:S(2)}, u32[]{:S(2)}) collective-permute-start(bf16[1024,256]{1,0:T(8,128)(2,1)S(1)} %bitcast.3), channel_id=1, source_target_pairs={{0,48},{1,17},{2,50},{3,19},{4,52},{5,21},{6,54},{7,23},{8,56},{9,... | collective-permute-start | bytes 1572872 | tf_op jit(solution)/shard_map/ppermute | solution.py:33
  25.1 3.4 %collective-permute-start.1 = (bf16[512,256]{1,0:T(8,128)(2,1)S(1)}, bf16[512,256]{1,0:T(8,128)(2,1)S(1)}, u32[]{:S(2)}, u32[]{:S(2)}) collective-permute-start(bf16[512,256]{1,0:T(8,128)(2,1)S(1)} %bitcast.6), channel_id=1, source_target_pairs={{0,16},{1,49},{2,18},{3,51},{4,20},{5,53},{6,22},{7,55},{8,24},{9,... | collective-permute-start | bytes 786440 | tf_op jit(solution)/shard_map/ppermute | solution.py:33
  28.5 3.2 %collective-permute-start.3 = (bf16[512,256]{1,0:T(8,128)(2,1)S(1)}, bf16[512,256]{1,0:T(8,128)(2,1)S(1)}, u32[]{:S(2)}, u32[]{:S(2)}) collective-permute-start(bf16[512,256]{1,0:T(8,128)(2,1)S(1)} %bitcast.5), channel_id=1, source_target_pairs={{0,16},{1,49},{2,18},{3,51},{4,20},{5,53},{6,22},{7,55},{8,24},{9,... | collective-permute-start | bytes 786440 | tf_op jit(solution)/shard_map/ppermute | solution.py:33
  31.7 0.0 collective-permute-done
  31.8 3.6 %collective-permute-done.1.refs_1_ = bf16[512,256]{1,0:T(8,128)(2,1)S(1)} collective-permute-done((bf16[512,256]{1,0:T(8,128)(2,1)S(1)}, bf16[512,256]{1,0:T(8,128)(2,1)S(1)}, u32[]{:S(2)}, u32[]{:S(2)}) %collective-permute-start.1) | collective-permute-done | bytes 262176 | tf_op jit(solution)/shard_map/ppermute | solution.py:33
  35.3 4.6 %collective-permute-start.2 = (bf16[512,256]{1,0:T(8,128)(2,1)S(1)}, bf16[512,256]{1,0:T(8,128)(2,1)S(1)}, u32[]{:S(2)}, u32[]{:S(2)}) collective-permute-start(bf16[512,256]{1,0:T(8,128)(2,1)S(1)} %collective-permute-done.1.refs_1_), channel_id=1, source_target_pairs={{0,16},{1,49},{2,18},{3,51},{4,20},{5,53},{6,22},{7,55},{8,24},{9,... | collective-permute-start | bytes 786440 | tf_op jit(solution)/shard_map/ppermute | solution.py:33
  39.9 0.0 collective-permute-done.3.refs_2_
  39.9 4.7 %collective-permute-start.4 = (bf16[512,256]{1,0:T(8,128)(2,1)S(1)}, bf16[512,256]{1,0:T(8,128)(2,1)S(1)}, u32[]{:S(2)}, u32[]{:S(2)}) collective-permute-start(bf16[512,256]{1,0:T(8,128)(2,1)S(1)} %collective-permute-done.3.refs_2_), channel_id=1, source_target_pairs={{0,16},{1,49},{2,18},{3,51},{4,20},{5,53},{6,22},{7,55},{8,24},{9,... | collective-permute-start | bytes 786440 | tf_op jit(solution)/shard_map/ppermute | solution.py:33
  44.6 2.9 %shard_map.37.refs_3_ = f32[8,144,256]{2,1,0:T(8,128)S(1)} custom-call(bf16[256,1024]{1,0:T(8,128)(2,1)S(1)} %constant_dynamic-update-slice_fusion.refs_0_, bf16[1024,256]{1,0:T(8,128)(2,1)S(1)} %bitcast.4), custom_call_target="tpu_custom_call" | custom-call | flops 1073741824 | bytes 1048576 | tf_op jit(solution)/shard_map/pallas_call | solution.py:162
  47.5 3.2 %shard_map.38.refs_2_ = f32[8,144,256]{2,1,0:T(8,128)S(1)} custom-call(bf16[256,1024]{1,0:T(8,128)(2,1)S(1)} %constant_dynamic-update-slice_fusion.refs_0_, bf16[512,256]{1,0:T(8,128)(2,1)S(1)} %collective-permute-done.1.refs_1_, bf16[512,256]{1,0:T(8,128)(2,1)S(1)} %collective-permute-done.3.refs_2_, ...), custom_call_target="tpu_custom_call", output_to_operand_aliasing={{}: (3, {})} | custom-call | flops 1073741824 | bytes 1048576 | tf_op jit(solution)/shard_map/pallas_call | solution.py:162
  50.7 0.0 collective-permute-done.5.refs_1_
  50.7 3.1 %shard_map.39 = (f32[4,144,256]{2,1,0:T(8,128)S(1)}, f32[4,144,256]{2,1,0:T(8,128)S(1)}) custom-call(bf16[256,1024]{1,0:T(8,128)(2,1)S(1)} %constant_dynamic-update-slice_fusion.refs_0_, bf16[1024,256]{1,0:T(8,128)(2,1)S(1)} %collective-permute-done.5.refs_1_, f32[8,144,256]{2,1,0:T(8,128)S(1)} %shard_map.38.refs_2_), custom_call_target="tpu_custom_call" | custom-call | flops 1073741824 | bytes 1048576 | tf_op jit(solution)/shard_map/pallas_call | solution.py:162
  53.8 0.0 collective-permute-done.2.refs_1_
  53.8 0.0 collective-permute-done.4.refs_2_
  53.8 1.8 %shard_map.41 = f32[4,144,256]{2,1,0:T(8,128)S(1)} custom-call(bf16[256,1024]{1,0:T(8,128)(2,1)S(1)} %constant_dynamic-update-slice_fusion.refs_0_, bf16[512,256]{1,0:T(8,128)(2,1)S(1)} %collective-permute-done.2.refs_1_, bf16[512,256]{1,0:T(8,128)(2,1)S(1)} %collective-permute-done.4.refs_2_, ...), custom_call_target="tpu_custom_call", output_to_operand_aliasing={{}: (3, {})} | custom-call | flops 536870912 | bytes 786432 | tf_op jit(solution)/shard_map/pallas_call | solution.py:162
  55.6 1.9 %collective-permute-start.6 = (f32[4,144,256]{2,1,0:T(8,128)S(1)}, f32[4,144,256]{2,1,0:T(8,128)S(1)}, u32[]{:S(2)}, u32[]{:S(2)}) collective-permute-start(f32[4,144,256]{2,1,0:T(8,128)S(1)} %shard_map.41), channel_id=1, source_target_pairs={{0,1},{1,0},{2,3},{3,2},{4,5},{5,4},{6,7},{7,6},{8,9},{9,8},{10,11... | collective-permute-start | bytes 1769480 | tf_op jit(solution)/shard_map/ppermute | solution.py:37
  57.5 1.8 %shard_map.40.mine_ref = f32[4,144,256]{2,1,0:T(8,128)S(1)} custom-call(bf16[256,1024]{1,0:T(8,128)(2,1)S(1)} %constant_dynamic-update-slice_fusion.refs_0_, bf16[512,256]{1,0:T(8,128)(2,1)S(1)} %collective-permute-done.2.refs_1_, bf16[512,256]{1,0:T(8,128)(2,1)S(1)} %collective-permute-done.4.refs_2_, ...), custom_call_target="tpu_custom_call", output_to_operand_aliasing={{}: (3, {})} | custom-call | flops 536870912 | bytes 786432 | tf_op jit(solution)/shard_map/pallas_call | solution.py:162
  59.3 0.2 collective-permute-done.6.theirs_ref
  59.5 0.9 %merge.1 = bf16[256,512]{1,0:T(8,128)(2,1)} custom-call(f32[4,144,256]{2,1,0:T(8,128)S(1)} %shard_map.40.mine_ref, f32[4,144,256]{2,1,0:T(8,128)S(1)} %collective-permute-done.6.theirs_ref), custom_call_target="tpu_custom_call" | custom-call | flops 1048576 | bytes 1048576 | tf_op jit(solution)/shard_map/merge/pallas_call | solution.py:224
  (3 shorter events, 0.1 us)
Async XLA Ops:
  0.0 8.1 %copy-start = (bf16[256,512]{1,0:T(8,128)(2,1)S(1)}, bf16[256,512]{1,0:T(8,128)(2,1)}, u32[]{:S(2)}) copy-start(bf16[256,512]{1,0:T(8,128)(2,1)} %param.3) | copy-start | bytes 786436
  1.7 20.3 %all-to-all-start = ((bf16[8,128,256]{2,1,0:T(8,128)(2,1)}), bf16[8,128,256]{2,1,0:T(8,128)(2,1)S(1)}, u32[]{:S(2)}, u32[]{:S(2)}) async-start(bf16[8,128,256]{2,1,0:T(8,128)(2,1)} %spread.1), calls=%async_computation | async-start | bytes 1048576 | tf_op jit(solution)/shard_map/all_to_all | solution.py:237
  8.1 23.6 %collective-permute-start = (bf16[256,512]{1,0:T(8,128)(2,1)S(1)}, bf16[256,512]{1,0:T(8,128)(2,1)S(1)}, u32[]{:S(2)}, u32[]{:S(2)}) collective-permute-start(bf16[256,512]{1,0:T(8,128)(2,1)S(1)} %copy-done), channel_id=1, source_target_pairs={{0,1},{1,0},{2,3},{3,2},{4,5},{5,4},{6,7},{7,6},{8,9},{9,8},{10,11... | collective-permute-start | bytes 786440 | tf_op jit(solution)/shard_map/ppermute | solution.py:37
  22.0 28.8 %collective-permute-start.5 = (bf16[1024,256]{1,0:T(8,128)(2,1)S(1)}, bf16[1024,256]{1,0:T(8,128)(2,1)S(1)}, u32[]{:S(2)}, u32[]{:S(2)}) collective-permute-start(bf16[1024,256]{1,0:T(8,128)(2,1)S(1)} %bitcast.3), channel_id=1, source_target_pairs={{0,48},{1,17},{2,50},{3,19},{4,52},{5,21},{6,54},{7,23},{8,56},{9,... | collective-permute-start | bytes 1572872 | tf_op jit(solution)/shard_map/ppermute | solution.py:33
  25.1 10.2 %collective-permute-start.1 = (bf16[512,256]{1,0:T(8,128)(2,1)S(1)}, bf16[512,256]{1,0:T(8,128)(2,1)S(1)}, u32[]{:S(2)}, u32[]{:S(2)}) collective-permute-start(bf16[512,256]{1,0:T(8,128)(2,1)S(1)} %bitcast.6), channel_id=1, source_target_pairs={{0,16},{1,49},{2,18},{3,51},{4,20},{5,53},{6,22},{7,55},{8,24},{9,... | collective-permute-start | bytes 786440 | tf_op jit(solution)/shard_map/ppermute | solution.py:33
  28.5 11.4 %collective-permute-start.3 = (bf16[512,256]{1,0:T(8,128)(2,1)S(1)}, bf16[512,256]{1,0:T(8,128)(2,1)S(1)}, u32[]{:S(2)}, u32[]{:S(2)}) collective-permute-start(bf16[512,256]{1,0:T(8,128)(2,1)S(1)} %bitcast.5), channel_id=1, source_target_pairs={{0,16},{1,49},{2,18},{3,51},{4,20},{5,53},{6,22},{7,55},{8,24},{9,... | collective-permute-start | bytes 786440 | tf_op jit(solution)/shard_map/ppermute | solution.py:33
  35.3 18.5 %collective-permute-start.2 = (bf16[512,256]{1,0:T(8,128)(2,1)S(1)}, bf16[512,256]{1,0:T(8,128)(2,1)S(1)}, u32[]{:S(2)}, u32[]{:S(2)}) collective-permute-start(bf16[512,256]{1,0:T(8,128)(2,1)S(1)} %collective-permute-done.1.refs_1_), channel_id=1, source_target_pairs={{0,16},{1,49},{2,18},{3,51},{4,20},{5,53},{6,22},{7,55},{8,24},{9,... | collective-permute-start | bytes 786440 | tf_op jit(solution)/shard_map/ppermute | solution.py:33
  39.9 13.9 %collective-permute-start.4 = (bf16[512,256]{1,0:T(8,128)(2,1)S(1)}, bf16[512,256]{1,0:T(8,128)(2,1)S(1)}, u32[]{:S(2)}, u32[]{:S(2)}) collective-permute-start(bf16[512,256]{1,0:T(8,128)(2,1)S(1)} %collective-permute-done.3.refs_2_), channel_id=1, source_target_pairs={{0,16},{1,49},{2,18},{3,51},{4,20},{5,53},{6,22},{7,55},{8,24},{9,... | collective-permute-start | bytes 786440 | tf_op jit(solution)/shard_map/ppermute | solution.py:33
  55.6 3.9 %collective-permute-start.6 = (f32[4,144,256]{2,1,0:T(8,128)S(1)}, f32[4,144,256]{2,1,0:T(8,128)S(1)}, u32[]{:S(2)}, u32[]{:S(2)}) collective-permute-start(f32[4,144,256]{2,1,0:T(8,128)S(1)} %shard_map.41), channel_id=1, source_target_pairs={{0,1},{1,0},{2,3},{3,2},{4,5},{5,4},{6,7},{7,6},{8,9},{9,8},{10,11... | collective-permute-start | bytes 1769480 | tf_op jit(solution)/shard_map/ppermute | solution.py:37

commit v3 on v2

--- a/solution.py
+++ b/solution.py
@@ -22,10 +22,10 @@
     return (((y % Y) * X + (x % X)) * Z + z) * C + c
 
 
-def move(a, first, second):
+def move(a, first, second, start=0):
     pairs = [
         (place(y, x, z, c), place(y, x + by, z, c))
-        for y in range(Y)
+        for y in range(start, Y)
         for x in range(X)
         for z in range(Z)
         for c, by in enumerate((first, second))
@@ -237,12 +237,12 @@
     own = lax.all_to_all(spread(keys, values), "ctx", 0, 0, axis_index_groups=groups).reshape(-1, 2 * HEAD_DIM)
     q = jnp.concatenate([queries, swap(queries)], 1)
     near = []
-    for rows in jnp.split(own, 2):
-        near.append(move(rows, 1, -1))
+    for n, rows in enumerate(jnp.split(own, 2)):
+        near.append(move(rows, 1, -1, n * (Y // 2)))
     other = move(own, -1, 1)
     far = []
-    for chunk in near:
-        far.append(move(chunk, 1, -1))
+    for n, chunk in enumerate(near):
+        far.append(move(chunk, 1, -1, n * (Y // 2)))
     state = run(0, q, [own])
     state = run(1, q, near, state)
     mine, theirs = run(-1, q, [other], state, n_out=2)

time: 60.7 us -> 60.7 us (level)
  no operation moved by 1% of the time
where the time goes in v3:
time: 60.7 us; the launch traced here: 60.4 us
  starting transfers between devices  30.4 us (50%)
  Pallas kernels  15.3 us (25%)
  waiting for transfers between devices  14.5 us (24%)
    ppermute x5, starting transfers between devices, move(): return lax.ppermute(a, ('ctx', 'tp'), pairs)  18.9 us
    pallas_call x5, Pallas kernels, run(): pl.pallas_call(functools.partial(kernel, shift, len(kvs), head_at, heads,...  12.7 us
    all_to_all x1, waiting for transfers between devices, shards(): lax.all_to_all(spread(keys, values), 'ctx', 0, 0, axis_index_groups=groups)  10.7 us
    all_to_all x1, starting transfers between devices, shards(): lax.all_to_all(spread(keys, values), 'ctx', 0, 0, axis_index_groups=groups)  6.43 us
    ppermute x2, starting transfers between devices, swap(): return lax.ppermute(a, 'tp', [(i, i ^ 1) for i in range(Z * C)])  5.05 us
    ppermute x5, waiting for transfers between devices, move(): return lax.ppermute(a, ('ctx', 'tp'), pairs)  3.59 us
    pallas_call x1, Pallas kernels, spread(): pl.pallas_call(spread_kernel, in_specs=[hbm, hbm], out_specs=hbm, out_sha...  1.69 us
  transfers between devices with their start and end apart: 8, of which 3 were waited for; matrix products, arithmetic and copies ran while one was open for 0% of the time, Pallas kernels for 18%

profile of v3, /device:TPU:241, one launch (start us, length us, event | category | flops | bytes accessed | tf_op | source)
XLA Modules:
  0.0 60.4 jit_solution(12361392009224464893)
XLA Ops:
  0.0 0.0 copy-start
  0.0 1.7 %spread.1 = bf16[8,128,256]{2,1,0:T(8,128)(2,1)} custom-call(bf16[256,1024]{1,0:T(8,128)(2,1)} %keys_ref.1, bf16[256,1024]{1,0:T(8,128)(2,1)} %values_ref.1), custom_call_target="tpu_custom_call" | custom-call | tf_op jit(solution)/shard_map/spread/pallas_call | solution.py:207
  1.7 6.4 %all-to-all-start = ((bf16[8,128,256]{2,1,0:T(8,128)(2,1)}), bf16[8,128,256]{2,1,0:T(8,128)(2,1)S(1)}, u32[]{:S(2)}, u32[]{:S(2)}) async-start(bf16[8,128,256]{2,1,0:T(8,128)(2,1)} %spread.1), calls=%async_computation | async-start | bytes 1048576 | tf_op jit(solution)/shard_map/all_to_all | solution.py:237
  8.1 0.0 copy-done
  8.1 3.1 %collective-permute-start = (bf16[256,512]{1,0:T(8,128)(2,1)S(1)}, bf16[256,512]{1,0:T(8,128)(2,1)S(1)}, u32[]{:S(2)}, u32[]{:S(2)}) collective-permute-start(bf16[256,512]{1,0:T(8,128)(2,1)S(1)} %copy-done), channel_id=1, source_target_pairs={{0,1},{1,0},{2,3},{3,2},{4,5},{5,4},{6,7},{7,6},{8,9},{9,8},{10,11... | collective-permute-start | bytes 786440 | tf_op jit(solution)/shard_map/ppermute | solution.py:37
  11.3 10.7 %all-to-all-done = bf16[8,128,256]{2,1,0:T(8,128)(2,1)S(1)} async-done(((bf16[8,128,256]{2,1,0:T(8,128)(2,1)}), bf16[8,128,256]{2,1,0:T(8,128)(2,1)S(1)}, u32[]{:S(2)}, u32[]{:S(2)}) %all-to-all-start) | async-done | bytes 524320 | tf_op jit(solution)/shard_map/all_to_all | solution.py:237
  22.0 3.1 %collective-permute-start.5 = (bf16[1024,256]{1,0:T(8,128)(2,1)S(1)}, bf16[1024,256]{1,0:T(8,128)(2,1)S(1)}, u32[]{:S(2)}, u32[]{:S(2)}) collective-permute-start(bf16[1024,256]{1,0:T(8,128)(2,1)S(1)} %bitcast.3), channel_id=1, source_target_pairs={{0,48},{1,17},{2,50},{3,19},{4,52},{5,21},{6,54},{7,23},{8,56},{9,... | collective-permute-start | bytes 1572872 | tf_op jit(solution)/shard_map/ppermute | solution.py:33
  25.1 3.4 %collective-permute-start.1 = (bf16[512,256]{1,0:T(8,128)(2,1)S(1)}, bf16[512,256]{1,0:T(8,128)(2,1)S(1)}, u32[]{:S(2)}, u32[]{:S(2)}) collective-permute-start(bf16[512,256]{1,0:T(8,128)(2,1)S(1)} %bitcast.6), channel_id=1, source_target_pairs={{0,16},{1,49},{2,18},{3,51},{4,20},{5,53},{6,22},{7,55},{8,24},{9,... | collective-permute-start | bytes 786440 | tf_op jit(solution)/shard_map/ppermute | solution.py:33
  28.5 3.2 %collective-permute-start.3 = (bf16[512,256]{1,0:T(8,128)(2,1)S(1)}, bf16[512,256]{1,0:T(8,128)(2,1)S(1)}, u32[]{:S(2)}, u32[]{:S(2)}) collective-permute-start(bf16[512,256]{1,0:T(8,128)(2,1)S(1)} %bitcast.5), channel_id=1, source_target_pairs={{256,272},{257,305},{258,274},{259,307},{260,276},{261,309},{262,2... | collective-permute-start | bytes 786440 | tf_op jit(solution)/shard_map/ppermute | solution.py:33
  31.7 0.0 collective-permute-done
  31.8 3.6 %collective-permute-done.1.refs_1_ = bf16[512,256]{1,0:T(8,128)(2,1)S(1)} collective-permute-done((bf16[512,256]{1,0:T(8,128)(2,1)S(1)}, bf16[512,256]{1,0:T(8,128)(2,1)S(1)}, u32[]{:S(2)}, u32[]{:S(2)}) %collective-permute-start.1) | collective-permute-done | bytes 262176 | tf_op jit(solution)/shard_map/ppermute | solution.py:33
  35.3 4.6 %collective-permute-start.2 = (bf16[512,256]{1,0:T(8,128)(2,1)S(1)}, bf16[512,256]{1,0:T(8,128)(2,1)S(1)}, u32[]{:S(2)}, u32[]{:S(2)}) collective-permute-start(bf16[512,256]{1,0:T(8,128)(2,1)S(1)} %collective-permute-done.1.refs_1_), channel_id=1, source_target_pairs={{0,16},{1,49},{2,18},{3,51},{4,20},{5,53},{6,22},{7,55},{8,24},{9,... | collective-permute-start | bytes 786440 | tf_op jit(solution)/shard_map/ppermute | solution.py:33
  39.9 0.0 collective-permute-done.3.refs_2_
  39.9 4.7 %collective-permute-start.4 = (bf16[512,256]{1,0:T(8,128)(2,1)S(1)}, bf16[512,256]{1,0:T(8,128)(2,1)S(1)}, u32[]{:S(2)}, u32[]{:S(2)}) collective-permute-start(bf16[512,256]{1,0:T(8,128)(2,1)S(1)} %collective-permute-done.3.refs_2_), channel_id=1, source_target_pairs={{256,272},{257,305},{258,274},{259,307},{260,276},{261,309},{262,2... | collective-permute-start | bytes 786440 | tf_op jit(solution)/shard_map/ppermute | solution.py:33
  44.6 2.9 %shard_map.37.refs_3_ = f32[8,144,256]{2,1,0:T(8,128)S(1)} custom-call(bf16[256,1024]{1,0:T(8,128)(2,1)S(1)} %constant_dynamic-update-slice_fusion.refs_0_, bf16[1024,256]{1,0:T(8,128)(2,1)S(1)} %bitcast.4), custom_call_target="tpu_custom_call" | custom-call | flops 1073741824 | bytes 1048576 | tf_op jit(solution)/shard_map/pallas_call | solution.py:162
  47.5 3.2 %shard_map.38.refs_2_ = f32[8,144,256]{2,1,0:T(8,128)S(1)} custom-call(bf16[256,1024]{1,0:T(8,128)(2,1)S(1)} %constant_dynamic-update-slice_fusion.refs_0_, bf16[512,256]{1,0:T(8,128)(2,1)S(1)} %collective-permute-done.1.refs_1_, bf16[512,256]{1,0:T(8,128)(2,1)S(1)} %collective-permute-done.3.refs_2_, ...), custom_call_target="tpu_custom_call", output_to_operand_aliasing={{}: (3, {})} | custom-call | flops 1073741824 | bytes 1048576 | tf_op jit(solution)/shard_map/pallas_call | solution.py:162
  50.7 0.0 collective-permute-done.5.refs_1_
  50.7 3.1 %shard_map.39 = (f32[4,144,256]{2,1,0:T(8,128)S(1)}, f32[4,144,256]{2,1,0:T(8,128)S(1)}) custom-call(bf16[256,1024]{1,0:T(8,128)(2,1)S(1)} %constant_dynamic-update-slice_fusion.refs_0_, bf16[1024,256]{1,0:T(8,128)(2,1)S(1)} %collective-permute-done.5.refs_1_, f32[8,144,256]{2,1,0:T(8,128)S(1)} %shard_map.38.refs_2_), custom_call_target="tpu_custom_call" | custom-call | flops 1073741824 | bytes 1048576 | tf_op jit(solution)/shard_map/pallas_call | solution.py:162
  53.8 0.0 collective-permute-done.2.refs_1_
  53.8 0.0 collective-permute-done.4.refs_2_
  53.8 1.8 %shard_map.41 = f32[4,144,256]{2,1,0:T(8,128)S(1)} custom-call(bf16[256,1024]{1,0:T(8,128)(2,1)S(1)} %constant_dynamic-update-slice_fusion.refs_0_, bf16[512,256]{1,0:T(8,128)(2,1)S(1)} %collective-permute-done.2.refs_1_, bf16[512,256]{1,0:T(8,128)(2,1)S(1)} %collective-permute-done.4.refs_2_, ...), custom_call_target="tpu_custom_call", output_to_operand_aliasing={{}: (3, {})} | custom-call | flops 536870912 | bytes 786432 | tf_op jit(solution)/shard_map/pallas_call | solution.py:162
  55.6 1.9 %collective-permute-start.6 = (f32[4,144,256]{2,1,0:T(8,128)S(1)}, f32[4,144,256]{2,1,0:T(8,128)S(1)}, u32[]{:S(2)}, u32[]{:S(2)}) collective-permute-start(f32[4,144,256]{2,1,0:T(8,128)S(1)} %shard_map.41), channel_id=1, source_target_pairs={{0,1},{1,0},{2,3},{3,2},{4,5},{5,4},{6,7},{7,6},{8,9},{9,8},{10,11... | collective-permute-start | bytes 1769480 | tf_op jit(solution)/shard_map/ppermute | solution.py:37
  57.5 1.8 %shard_map.40.mine_ref = f32[4,144,256]{2,1,0:T(8,128)S(1)} custom-call(bf16[256,1024]{1,0:T(8,128)(2,1)S(1)} %constant_dynamic-update-slice_fusion.refs_0_, bf16[512,256]{1,0:T(8,128)(2,1)S(1)} %collective-permute-done.2.refs_1_, bf16[512,256]{1,0:T(8,128)(2,1)S(1)} %collective-permute-done.4.refs_2_, ...), custom_call_target="tpu_custom_call", output_to_operand_aliasing={{}: (3, {})} | custom-call | flops 536870912 | bytes 786432 | tf_op jit(solution)/shard_map/pallas_call | solution.py:162
  59.3 0.2 collective-permute-done.6.theirs_ref
  59.5 0.9 %merge.1 = bf16[256,512]{1,0:T(8,128)(2,1)} custom-call(f32[4,144,256]{2,1,0:T(8,128)S(1)} %shard_map.40.mine_ref, f32[4,144,256]{2,1,0:T(8,128)S(1)} %collective-permute-done.6.theirs_ref), custom_call_target="tpu_custom_call" | custom-call | flops 1048576 | bytes 1048576 | tf_op jit(solution)/shard_map/merge/pallas_call | solution.py:224
  (3 shorter events, 0.1 us)
Async XLA Ops:
  0.0 8.1 %copy-start = (bf16[256,512]{1,0:T(8,128)(2,1)S(1)}, bf16[256,512]{1,0:T(8,128)(2,1)}, u32[]{:S(2)}) copy-start(bf16[256,512]{1,0:T(8,128)(2,1)} %param.3) | copy-start | bytes 786436
  1.7 20.3 %all-to-all-start = ((bf16[8,128,256]{2,1,0:T(8,128)(2,1)}), bf16[8,128,256]{2,1,0:T(8,128)(2,1)S(1)}, u32[]{:S(2)}, u32[]{:S(2)}) async-start(bf16[8,128,256]{2,1,0:T(8,128)(2,1)} %spread.1), calls=%async_computation | async-start | bytes 1048576 | tf_op jit(solution)/shard_map/all_to_all | solution.py:237
  8.1 23.6 %collective-permute-start = (bf16[256,512]{1,0:T(8,128)(2,1)S(1)}, bf16[256,512]{1,0:T(8,128)(2,1)S(1)}, u32[]{:S(2)}, u32[]{:S(2)}) collective-permute-start(bf16[256,512]{1,0:T(8,128)(2,1)S(1)} %copy-done), channel_id=1, source_target_pairs={{0,1},{1,0},{2,3},{3,2},{4,5},{5,4},{6,7},{7,6},{8,9},{9,8},{10,11... | collective-permute-start | bytes 786440 | tf_op jit(solution)/shard_map/ppermute | solution.py:37
  22.0 28.8 %collective-permute-start.5 = (bf16[1024,256]{1,0:T(8,128)(2,1)S(1)}, bf16[1024,256]{1,0:T(8,128)(2,1)S(1)}, u32[]{:S(2)}, u32[]{:S(2)}) collective-permute-start(bf16[1024,256]{1,0:T(8,128)(2,1)S(1)} %bitcast.3), channel_id=1, source_target_pairs={{0,48},{1,17},{2,50},{3,19},{4,52},{5,21},{6,54},{7,23},{8,56},{9,... | collective-permute-start | bytes 1572872 | tf_op jit(solution)/shard_map/ppermute | solution.py:33
  25.1 10.2 %collective-permute-start.1 = (bf16[512,256]{1,0:T(8,128)(2,1)S(1)}, bf16[512,256]{1,0:T(8,128)(2,1)S(1)}, u32[]{:S(2)}, u32[]{:S(2)}) collective-permute-start(bf16[512,256]{1,0:T(8,128)(2,1)S(1)} %bitcast.6), channel_id=1, source_target_pairs={{0,16},{1,49},{2,18},{3,51},{4,20},{5,53},{6,22},{7,55},{8,24},{9,... | collective-permute-start | bytes 786440 | tf_op jit(solution)/shard_map/ppermute | solution.py:33
  28.5 11.4 %collective-permute-start.3 = (bf16[512,256]{1,0:T(8,128)(2,1)S(1)}, bf16[512,256]{1,0:T(8,128)(2,1)S(1)}, u32[]{:S(2)}, u32[]{:S(2)}) collective-permute-start(bf16[512,256]{1,0:T(8,128)(2,1)S(1)} %bitcast.5), channel_id=1, source_target_pairs={{256,272},{257,305},{258,274},{259,307},{260,276},{261,309},{262,2... | collective-permute-start | bytes 786440 | tf_op jit(solution)/shard_map/ppermute | solution.py:33
  35.3 18.5 %collective-permute-start.2 = (bf16[512,256]{1,0:T(8,128)(2,1)S(1)}, bf16[512,256]{1,0:T(8,128)(2,1)S(1)}, u32[]{:S(2)}, u32[]{:S(2)}) collective-permute-start(bf16[512,256]{1,0:T(8,128)(2,1)S(1)} %collective-permute-done.1.refs_1_), channel_id=1, source_target_pairs={{0,16},{1,49},{2,18},{3,51},{4,20},{5,53},{6,22},{7,55},{8,24},{9,... | collective-permute-start | bytes 786440 | tf_op jit(solution)/shard_map/ppermute | solution.py:33
  39.9 13.9 %collective-permute-start.4 = (bf16[512,256]{1,0:T(8,128)(2,1)S(1)}, bf16[512,256]{1,0:T(8,128)(2,1)S(1)}, u32[]{:S(2)}, u32[]{:S(2)}) collective-permute-start(bf16[512,256]{1,0:T(8,128)(2,1)S(1)} %collective-permute-done.3.refs_2_), channel_id=1, source_target_pairs={{256,272},{257,305},{258,274},{259,307},{260,276},{261,309},{262,2... | collective-permute-start | bytes 786440 | tf_op jit(solution)/shard_map/ppermute | solution.py:33
  55.6 3.9 %collective-permute-start.6 = (f32[4,144,256]{2,1,0:T(8,128)S(1)}, f32[4,144,256]{2,1,0:T(8,128)S(1)}, u32[]{:S(2)}, u32[]{:S(2)}) collective-permute-start(f32[4,144,256]{2,1,0:T(8,128)S(1)} %shard_map.41), channel_id=1, source_target_pairs={{0,1},{1,0},{2,3},{3,2},{4,5},{5,4},{6,7},{7,6},{8,9},{9,8},{10,11... | collective-permute-start | bytes 1769480 | tf_op jit(solution)/shard_map/ppermute | solution.py:37

commit v4 on v3

--- a/solution.py
+++ b/solution.py
@@ -13,6 +13,7 @@
 HEAD_DIM = 128
 GROUP = HEADS // KV_HEADS
 Y, X, Z, C = 8, 4, 8, 2
+STEPS = (4, 6, 8)
 MASKED, EMPTY = -1e30, -1e29
 EXPONENT = HEAD_DIM**-0.5 * 1.4426950408889634
 TOTAL, PEAK, ROWS = HEAD_DIM, HEAD_DIM + 8, HEAD_DIM + 16
@@ -37,12 +38,12 @@
     return lax.ppermute(a, "tp", [(i, i ^ 1) for i in range(Z * C)])
 
 
-def absorb(q_ref, kv_refs, count, delta, masks, head_at, heads, state_in, outs, scores_ref, weights_ref, values_ref):
+def absorb(q_ref, kv_refs, from_row, count, delta, masks, head_at, heads, state_in, outs, scores_ref, weights_ref, values_ref):
     rows = q_ref.shape[0]
     sub = rows // C
     size = kv_refs[0].shape[0]
     parts = [
-        (kv_refs[at // size], at % size, at // sub * (X * rows), masks[0] <= at < masks[1])
+        (kv_refs[at // size], at % size, (from_row + at // sub) * (X * rows), at >= masks)
         for at in range(0, count, sub)
     ]
     total = len(parts) * sub
@@ -101,10 +102,11 @@
     from_x = lax.rem(x + shift * (toward if abs(shift) == 1 else 1) + X, X)
     delta = (from_x - x - y * X) * rows + core * (rows // 2)
     needed = y + jnp.where(delta + y * X * rows < rows, 1, 0)
-    return jnp.where(needed == 0, 0, jnp.where(needed <= Y // 2, 1, 2)), delta
-
-
-def kernel(shift, n_kv, head_at, heads, first, n_out, *refs):
+    amount = sum(jnp.where(needed > n, 1, 0) for n in (0,) + STEPS[:-1])
+    return amount, delta
+
+
+def kernel(shift, n_kv, from_row, head_at, heads, first, n_out, *refs):
     q_ref, kv_refs = refs[0], refs[1 : 1 + n_kv]
     n = 1 + n_kv
     amount, delta = needs(shift, q_ref.shape[0])
@@ -115,8 +117,7 @@
         n += 1
     outs, scratch = refs[n : n + n_out], refs[n + n_out :]
 
-    @pl.when(amount == 0)
-    def _():
+    def keep():
         for h in range(heads):
             per = heads // n_out
             ref, k = outs[h // per], h % per
@@ -126,12 +127,16 @@
             else:
                 ref[k] = state_in[h]
 
-    for n, count, masks in ((1, every // 2, (0, every)), (2, every, (every // 2, every))):
-        pl.when(amount == n)(
-            functools.partial(
-                absorb, q_ref, kv_refs, count, delta, masks, head_at, heads, state_in, outs, *scratch
+    sub = q_ref.shape[0] // C
+    for n, needed in enumerate((0,) + STEPS):
+        count = min((needed - from_row) * sub, every)
+        masks = (STEPS[n - 2] - from_row) * sub if n > 1 else 0
+        act = keep
+        if count > 0:
+            act = functools.partial(
+                absorb, q_ref, kv_refs, from_row, count, delta, masks, head_at, heads, state_in, outs, *scratch
             )
-        )
+        pl.when(amount == n)(act)
 
 
 def merge_kernel(mine_ref, theirs_ref, out_ref):
@@ -146,21 +151,21 @@
         normed = mine_ref[h, :HEAD_DIM].reshape(tiles) * (w * scale)[None] + theirs_ref[h, :HEAD_DIM].reshape(
             tiles
         ) * (w2 * scale)[None]
-        out_ref[:, h * HEAD_DIM : (h + 1) * HEAD_DIM] = normed.reshape(HEAD_DIM, rows).T.astype(jnp.bfloat16)
+        out_ref[:, h * HEAD_DIM : (h + 1) * HEAD_DIM] = normed.reshape(HEAD_DIM, rows).astype(jnp.bfloat16).T
 
 
 VMEM = pl.BlockSpec(memory_space=pltpu.VMEM)
 LIMIT = pltpu.CompilerParams(vmem_limit_bytes=24 * 2**20)
 
 
-def run(shift, q, kvs, state=None, n_out=1, head_at=0):
+def run(shift, q, kvs, state=None, n_out=1, head_at=0, from_row=0):
     rows = q.shape[0]
     heads = GROUP if state is None else state.shape[0]
     keys = sum(kv.shape[0] for kv in kvs)
     first = state is None
     shape = pltpu.VMEM((heads // n_out, ROWS, rows), jnp.float32)
     return pl.pallas_call(
-        functools.partial(kernel, shift, len(kvs), head_at, heads, first, n_out),
+        functools.partial(kernel, shift, len(kvs), from_row, head_at, heads, first, n_out),
         out_shape=shape if n_out == 1 else (shape,) * n_out,
         in_specs=[VMEM] * (1 + len(kvs) + (not first)),
         out_specs=VMEM if n_out == 1 else (VMEM,) * n_out,
@@ -245,10 +250,11 @@
         far.append(move(chunk, 1, -1, n * (Y // 2)))
     state = run(0, q, [own])
     state = run(1, q, near, state)
-    mine, theirs = run(-1, q, [other], state, n_out=2)
-    theirs = run(2, q, far, theirs, head_at=GROUP // 2)
+    state = run(-1, q, [other], state)
+    mine, theirs = run(2, q, far[:1], state, n_out=2)
+    theirs = run(2, q, far[1:], theirs, head_at=GROUP // 2, from_row=Y // 2)
     theirs = swap(theirs)
-    mine = run(2, q, far, mine)
+    mine = run(2, q, far[1:], mine, from_row=Y // 2)
     return merge(mine, theirs)
 
 

time: 60.7 us -> 60.9 us (level)
  the two profiles are of different devices: /device:TPU:241 before, /device:TPU:305 now
where the time goes in v4:
time: 60.9 us; the launch traced here: 60.5 us
  starting transfers between devices  30.4 us (50%)
  waiting for transfers between devices  15.5 us (25%)
  Pallas kernels  14.4 us (24%)
    ppermute x5, starting transfers between devices, move(): return lax.ppermute(a, ('ctx', 'tp'), pairs)  18.9 us
    pallas_call x6, Pallas kernels, run(): pl.pallas_call(functools.partial(kernel, shift, len(kvs), from_row, head_...  11.9 us
    all_to_all x1, waiting for transfers between devices, shards(): lax.all_to_all(spread(keys, values), 'ctx', 0, 0, axis_index_groups=groups)  10.7 us
    all_to_all x1, starting transfers between devices, shards(): lax.all_to_all(spread(keys, values), 'ctx', 0, 0, axis_index_groups=groups)  6.43 us
    ppermute x2, starting transfers between devices, swap(): return lax.ppermute(a, 'tp', [(i, i ^ 1) for i in range(Z * C)])  5.05 us
    ppermute x5, waiting for transfers between devices, move(): return lax.ppermute(a, ('ctx', 'tp'), pairs)  3.59 us
    pallas_call x1, Pallas kernels, spread(): pl.pallas_call(spread_kernel, in_specs=[hbm, hbm], out_specs=hbm, out_sha...  1.69 us
  transfers between devices with their start and end apart: 8, of which 3 were waited for; matrix products, arithmetic and copies ran while one was open for 0% of the time, Pallas kernels for 18%

profile of v4, /device:TPU:305, one launch (start us, length us, event | category | flops | bytes accessed | tf_op | source)
XLA Modules:
  0.0 60.5 jit_solution(2911215369501831068)
XLA Ops:
  0.0 0.0 copy-start
  0.0 1.7 %spread.1 = bf16[8,128,256]{2,1,0:T(8,128)(2,1)} custom-call(bf16[256,1024]{1,0:T(8,128)(2,1)} %keys_ref.1, bf16[256,1024]{1,0:T(8,128)(2,1)} %values_ref.1), custom_call_target="tpu_custom_call" | custom-call | tf_op jit(solution)/shard_map/spread/pallas_call | solution.py:212
  1.7 6.4 %all-to-all-start = ((bf16[8,128,256]{2,1,0:T(8,128)(2,1)}), bf16[8,128,256]{2,1,0:T(8,128)(2,1)S(1)}, u32[]{:S(2)}, u32[]{:S(2)}) async-start(bf16[8,128,256]{2,1,0:T(8,128)(2,1)} %spread.1), calls=%async_computation | async-start | bytes 1048576 | tf_op jit(solution)/shard_map/all_to_all | solution.py:242
  8.1 0.0 copy-done
  8.1 3.1 %collective-permute-start = (bf16[256,512]{1,0:T(8,128)(2,1)S(1)}, bf16[256,512]{1,0:T(8,128)(2,1)S(1)}, u32[]{:S(2)}, u32[]{:S(2)}) collective-permute-start(bf16[256,512]{1,0:T(8,128)(2,1)S(1)} %copy-done), channel_id=1, source_target_pairs={{0,1},{1,0},{2,3},{3,2},{4,5},{5,4},{6,7},{7,6},{8,9},{9,8},{10,11... | collective-permute-start | bytes 786440 | tf_op jit(solution)/shard_map/ppermute | solution.py:38
  11.3 10.7 %all-to-all-done = bf16[8,128,256]{2,1,0:T(8,128)(2,1)S(1)} async-done(((bf16[8,128,256]{2,1,0:T(8,128)(2,1)}), bf16[8,128,256]{2,1,0:T(8,128)(2,1)S(1)}, u32[]{:S(2)}, u32[]{:S(2)}) %all-to-all-start) | async-done | bytes 524320 | tf_op jit(solution)/shard_map/all_to_all | solution.py:242
  22.0 3.1 %collective-permute-start.5 = (bf16[1024,256]{1,0:T(8,128)(2,1)S(1)}, bf16[1024,256]{1,0:T(8,128)(2,1)S(1)}, u32[]{:S(2)}, u32[]{:S(2)}) collective-permute-start(bf16[1024,256]{1,0:T(8,128)(2,1)S(1)} %bitcast.3), channel_id=1, source_target_pairs={{0,48},{1,17},{2,50},{3,19},{4,52},{5,21},{6,54},{7,23},{8,56},{9,... | collective-permute-start | bytes 1572872 | tf_op jit(solution)/shard_map/ppermute | solution.py:34
  25.1 3.4 %collective-permute-start.3 = (bf16[512,256]{1,0:T(8,128)(2,1)S(1)}, bf16[512,256]{1,0:T(8,128)(2,1)S(1)}, u32[]{:S(2)}, u32[]{:S(2)}) collective-permute-start(bf16[512,256]{1,0:T(8,128)(2,1)S(1)} %bitcast.6), channel_id=1, source_target_pairs={{0,16},{1,49},{2,18},{3,51},{4,20},{5,53},{6,22},{7,55},{8,24},{9,... | collective-permute-start | bytes 786440 | tf_op jit(solution)/shard_map/ppermute | solution.py:34
  28.5 3.2 %collective-permute-start.1 = (bf16[512,256]{1,0:T(8,128)(2,1)S(1)}, bf16[512,256]{1,0:T(8,128)(2,1)S(1)}, u32[]{:S(2)}, u32[]{:S(2)}) collective-permute-start(bf16[512,256]{1,0:T(8,128)(2,1)S(1)} %bitcast.5), channel_id=1, source_target_pairs={{256,272},{257,305},{258,274},{259,307},{260,276},{261,309},{262,2... | collective-permute-start | bytes 786440 | tf_op jit(solution)/shard_map/ppermute | solution.py:34
  31.7 0.0 collective-permute-done
  31.8 3.6 %collective-permute-done.3.refs_1_ = bf16[512,256]{1,0:T(8,128)(2,1)S(1)} collective-permute-done((bf16[512,256]{1,0:T(8,128)(2,1)S(1)}, bf16[512,256]{1,0:T(8,128)(2,1)S(1)}, u32[]{:S(2)}, u32[]{:S(2)}) %collective-permute-start.3) | collective-permute-done | bytes 262176 | tf_op jit(solution)/shard_map/ppermute | solution.py:34
  35.3 4.6 %collective-permute-start.4 = (bf16[512,256]{1,0:T(8,128)(2,1)S(1)}, bf16[512,256]{1,0:T(8,128)(2,1)S(1)}, u32[]{:S(2)}, u32[]{:S(2)}) collective-permute-start(bf16[512,256]{1,0:T(8,128)(2,1)S(1)} %collective-permute-done.3.refs_1_), channel_id=1, source_target_pairs={{0,16},{1,49},{2,18},{3,51},{4,20},{5,53},{6,22},{7,55},{8,24},{9,... | collective-permute-start | bytes 786440 | tf_op jit(solution)/shard_map/ppermute | solution.py:34
  39.9 0.0 collective-permute-done.1.refs_2_
  39.9 4.7 %collective-permute-start.2 = (bf16[512,256]{1,0:T(8,128)(2,1)S(1)}, bf16[512,256]{1,0:T(8,128)(2,1)S(1)}, u32[]{:S(2)}, u32[]{:S(2)}) collective-permute-start(bf16[512,256]{1,0:T(8,128)(2,1)S(1)} %collective-permute-done.1.refs_2_), channel_id=1, source_target_pairs={{256,272},{257,305},{258,274},{259,307},{260,276},{261,309},{262,2... | collective-permute-start | bytes 786440 | tf_op jit(solution)/shard_map/ppermute | solution.py:34
  44.6 2.9 %shard_map.37.refs_3_ = f32[8,144,256]{2,1,0:T(8,128)S(1)} custom-call(bf16[256,1024]{1,0:T(8,128)(2,1)S(1)} %constant_dynamic-update-slice_fusion.refs_0_, bf16[1024,256]{1,0:T(8,128)(2,1)S(1)} %bitcast.4), custom_call_target="tpu_custom_call" | custom-call | flops 1073741824 | bytes 1048576 | tf_op jit(solution)/shard_map/pallas_call | solution.py:167
  47.5 2.8 %shard_map.38.refs_2_ = f32[8,144,256]{2,1,0:T(8,128)S(1)} custom-call(bf16[256,1024]{1,0:T(8,128)(2,1)S(1)} %constant_dynamic-update-slice_fusion.refs_0_, bf16[512,256]{1,0:T(8,128)(2,1)S(1)} %collective-permute-done.3.refs_1_, bf16[512,256]{1,0:T(8,128)(2,1)S(1)} %collective-permute-done.1.refs_2_, ...), custom_call_target="tpu_custom_call", output_to_operand_aliasing={{}: (3, {})} | custom-call | flops 1073741824 | bytes 1048576 | tf_op jit(solution)/shard_map/pallas_call | solution.py:167
  50.3 0.0 collective-permute-done.5.refs_1_
  50.4 2.7 %shard_map.39.refs_2_ = f32[8,144,256]{2,1,0:T(8,128)S(1)} custom-call(bf16[256,1024]{1,0:T(8,128)(2,1)S(1)} %constant_dynamic-update-slice_fusion.refs_0_, bf16[1024,256]{1,0:T(8,128)(2,1)S(1)} %collective-permute-done.5.refs_1_, f32[8,144,256]{2,1,0:T(8,128)S(1)} %shard_map.38.refs_2_), custom_call_target="tpu_custom_call", output_to_operand_aliasing={{}: (2, {})} | custom-call | flops 1073741824 | bytes 1048576 | tf_op jit(solution)/shard_map/pallas_call | solution.py:167
  53.0 0.0 collective-permute-done.4.refs_1_
  53.0 1.9 %shard_map.40 = (f32[4,144,256]{2,1,0:T(8,128)S(1)}, f32[4,144,256]{2,1,0:T(8,128)S(1)}) custom-call(bf16[256,1024]{1,0:T(8,128)(2,1)S(1)} %constant_dynamic-update-slice_fusion.refs_0_, bf16[512,256]{1,0:T(8,128)(2,1)S(1)} %collective-permute-done.4.refs_1_, f32[8,144,256]{2,1,0:T(8,128)S(1)} %shard_map.39.refs_2_), custom_call_target="tpu_custom_call" | custom-call | flops 536870912 | bytes 786432 | tf_op jit(solution)/shard_map/pallas_call | solution.py:167
  55.0 0.0 collective-permute-done.2.refs_1_
  55.0 0.8 %shard_map.42 = f32[4,144,256]{2,1,0:T(8,128)S(1)} custom-call(bf16[256,1024]{1,0:T(8,128)(2,1)S(1)} %constant_dynamic-update-slice_fusion.refs_0_, bf16[512,256]{1,0:T(8,128)(2,1)S(1)} %collective-permute-done.2.refs_1_, f32[4,144,256]{2,1,0:T(8,128)S(1)} %get-tuple-element.8.refs_2_), custom_call_target="tpu_custom_call", output_to_operand_aliasing={{}: (2, {})} | custom-call | flops 268435456 | bytes 524288 | tf_op jit(solution)/shard_map/pallas_call | solution.py:167
  55.8 1.9 %collective-permute-start.6 = (f32[4,144,256]{2,1,0:T(8,128)S(1)}, f32[4,144,256]{2,1,0:T(8,128)S(1)}, u32[]{:S(2)}, u32[]{:S(2)}) collective-permute-start(f32[4,144,256]{2,1,0:T(8,128)S(1)} %shard_map.42), channel_id=1, source_target_pairs={{0,1},{1,0},{2,3},{3,2},{4,5},{5,4},{6,7},{7,6},{8,9},{9,8},{10,11... | collective-permute-start | bytes 1769480 | tf_op jit(solution)/shard_map/ppermute | solution.py:38
  57.7 0.8 %shard_map.41.mine_ref = f32[4,144,256]{2,1,0:T(8,128)S(1)} custom-call(bf16[256,1024]{1,0:T(8,128)(2,1)S(1)} %constant_dynamic-update-slice_fusion.refs_0_, bf16[512,256]{1,0:T(8,128)(2,1)S(1)} %collective-permute-done.2.refs_1_, f32[4,144,256]{2,1,0:T(8,128)S(1)} %get-tuple-element.7.refs_2_), custom_call_target="tpu_custom_call", output_to_operand_aliasing={{}: (2, {})} | custom-call | flops 268435456 | bytes 524288 | tf_op jit(solution)/shard_map/pallas_call | solution.py:167
  58.5 1.2 %collective-permute-done.6.theirs_ref = f32[4,144,256]{2,1,0:T(8,128)S(1)} collective-permute-done((f32[4,144,256]{2,1,0:T(8,128)S(1)}, f32[4,144,256]{2,1,0:T(8,128)S(1)}, u32[]{:S(2)}, u32[]{:S(2)}) %collective-permute-start.6) | collective-permute-done | bytes 589856 | tf_op jit(solution)/shard_map/ppermute | solution.py:38
  59.7 0.9 %merge.1 = bf16[256,512]{1,0:T(8,128)(2,1)} custom-call(f32[4,144,256]{2,1,0:T(8,128)S(1)} %shard_map.41.mine_ref, f32[4,144,256]{2,1,0:T(8,128)S(1)} %collective-permute-done.6.theirs_ref), custom_call_target="tpu_custom_call" | custom-call | flops 1048576 | bytes 1048576 | tf_op jit(solution)/shard_map/merge/pallas_call | solution.py:229
  (3 shorter events, 0.1 us)
Async XLA Ops:
  0.0 8.1 %copy-start = (bf16[256,512]{1,0:T(8,128)(2,1)S(1)}, bf16[256,512]{1,0:T(8,128)(2,1)}, u32[]{:S(2)}) copy-start(bf16[256,512]{1,0:T(8,128)(2,1)} %param.3) | copy-start | bytes 786436
  1.7 20.3 %all-to-all-start = ((bf16[8,128,256]{2,1,0:T(8,128)(2,1)}), bf16[8,128,256]{2,1,0:T(8,128)(2,1)S(1)}, u32[]{:S(2)}, u32[]{:S(2)}) async-start(bf16[8,128,256]{2,1,0:T(8,128)(2,1)} %spread.1), calls=%async_computation | async-start | bytes 1048576 | tf_op jit(solution)/shard_map/all_to_all | solution.py:242
  8.1 23.6 %collective-permute-start = (bf16[256,512]{1,0:T(8,128)(2,1)S(1)}, bf16[256,512]{1,0:T(8,128)(2,1)S(1)}, u32[]{:S(2)}, u32[]{:S(2)}) collective-permute-start(bf16[256,512]{1,0:T(8,128)(2,1)S(1)} %copy-done), channel_id=1, source_target_pairs={{0,1},{1,0},{2,3},{3,2},{4,5},{5,4},{6,7},{7,6},{8,9},{9,8},{10,11... | collective-permute-start | bytes 786440 | tf_op jit(solution)/shard_map/ppermute | solution.py:38
  22.0 28.4 %collective-permute-start.5 = (bf16[1024,256]{1,0:T(8,128)(2,1)S(1)}, bf16[1024,256]{1,0:T(8,128)(2,1)S(1)}, u32[]{:S(2)}, u32[]{:S(2)}) collective-permute-start(bf16[1024,256]{1,0:T(8,128)(2,1)S(1)} %bitcast.3), channel_id=1, source_target_pairs={{0,48},{1,17},{2,50},{3,19},{4,52},{5,21},{6,54},{7,23},{8,56},{9,... | collective-permute-start | bytes 1572872 | tf_op jit(solution)/shard_map/ppermute | solution.py:34
  25.1 10.2 %collective-permute-start.3 = (bf16[512,256]{1,0:T(8,128)(2,1)S(1)}, bf16[512,256]{1,0:T(8,128)(2,1)S(1)}, u32[]{:S(2)}, u32[]{:S(2)}) collective-permute-start(bf16[512,256]{1,0:T(8,128)(2,1)S(1)} %bitcast.6), channel_id=1, source_target_pairs={{0,16},{1,49},{2,18},{3,51},{4,20},{5,53},{6,22},{7,55},{8,24},{9,... | collective-permute-start | bytes 786440 | tf_op jit(solution)/shard_map/ppermute | solution.py:34
  28.5 11.4 %collective-permute-start.1 = (bf16[512,256]{1,0:T(8,128)(2,1)S(1)}, bf16[512,256]{1,0:T(8,128)(2,1)S(1)}, u32[]{:S(2)}, u32[]{:S(2)}) collective-permute-start(bf16[512,256]{1,0:T(8,128)(2,1)S(1)} %bitcast.5), channel_id=1, source_target_pairs={{256,272},{257,305},{258,274},{259,307},{260,276},{261,309},{262,2... | collective-permute-start | bytes 786440 | tf_op jit(solution)/shard_map/ppermute | solution.py:34
  35.3 17.7 %collective-permute-start.4 = (bf16[512,256]{1,0:T(8,128)(2,1)S(1)}, bf16[512,256]{1,0:T(8,128)(2,1)S(1)}, u32[]{:S(2)}, u32[]{:S(2)}) collective-permute-start(bf16[512,256]{1,0:T(8,128)(2,1)S(1)} %collective-permute-done.3.refs_1_), channel_id=1, source_target_pairs={{0,16},{1,49},{2,18},{3,51},{4,20},{5,53},{6,22},{7,55},{8,24},{9,... | collective-permute-start | bytes 786440 | tf_op jit(solution)/shard_map/ppermute | solution.py:34
  39.9 15.1 %collective-permute-start.2 = (bf16[512,256]{1,0:T(8,128)(2,1)S(1)}, bf16[512,256]{1,0:T(8,128)(2,1)S(1)}, u32[]{:S(2)}, u32[]{:S(2)}) collective-permute-start(bf16[512,256]{1,0:T(8,128)(2,1)S(1)} %collective-permute-done.1.refs_2_), channel_id=1, source_target_pairs={{256,272},{257,305},{258,274},{259,307},{260,276},{261,309},{262,2... | collective-permute-start | bytes 786440 | tf_op jit(solution)/shard_map/ppermute | solution.py:34
  55.8 3.9 %collective-permute-start.6 = (f32[4,144,256]{2,1,0:T(8,128)S(1)}, f32[4,144,256]{2,1,0:T(8,128)S(1)}, u32[]{:S(2)}, u32[]{:S(2)}) collective-permute-start(f32[4,144,256]{2,1,0:T(8,128)S(1)} %shard_map.42), channel_id=1, source_target_pairs={{0,1},{1,0},{2,3},{3,2},{4,5},{5,4},{6,7},{7,6},{8,9},{9,8},{10,11... | collective-permute-start | bytes 1769480 | tf_op jit(solution)/shard_map/ppermute | solution.py:38

commit v5 on v3

--- a/solution.py
+++ b/solution.py
@@ -13,6 +13,7 @@
 HEAD_DIM = 128
 GROUP = HEADS // KV_HEADS
 Y, X, Z, C = 8, 4, 8, 2
+STEPS = (4, 6, 8)
 MASKED, EMPTY = -1e30, -1e29
 EXPONENT = HEAD_DIM**-0.5 * 1.4426950408889634
 TOTAL, PEAK, ROWS = HEAD_DIM, HEAD_DIM + 8, HEAD_DIM + 16
@@ -101,7 +102,8 @@
     from_x = lax.rem(x + shift * (toward if abs(shift) == 1 else 1) + X, X)
     delta = (from_x - x - y * X) * rows + core * (rows // 2)
     needed = y + jnp.where(delta + y * X * rows < rows, 1, 0)
-    return jnp.where(needed == 0, 0, jnp.where(needed <= Y // 2, 1, 2)), delta
+    amount = sum(jnp.where(needed > n, 1, 0) for n in (0,) + STEPS[:-1])
+    return amount, delta
 
 
 def kernel(shift, n_kv, head_at, heads, first, n_out, *refs):
@@ -126,8 +128,10 @@
             else:
                 ref[k] = state_in[h]
 
-    for n, count, masks in ((1, every // 2, (0, every)), (2, every, (every // 2, every))):
-        pl.when(amount == n)(
+    for n, last in enumerate(STEPS):
+        first_masked = STEPS[n - 1] if n else 0
+        count, masks = every // Y * last, (every // Y * first_masked, every)
+        pl.when(amount == n + 1)(
             functools.partial(
                 absorb, q_ref, kv_refs, count, delta, masks, head_at, heads, state_in, outs, *scratch
             )
@@ -146,11 +150,12 @@
         normed = mine_ref[h, :HEAD_DIM].reshape(tiles) * (w * scale)[None] + theirs_ref[h, :HEAD_DIM].reshape(
             tiles
         ) * (w2 * scale)[None]
-        out_ref[:, h * HEAD_DIM : (h + 1) * HEAD_DIM] = normed.reshape(HEAD_DIM, rows).T.astype(jnp.bfloat16)
+        out_ref[:, h * HEAD_DIM : (h + 1) * HEAD_DIM] = normed.reshape(HEAD_DIM, rows).astype(jnp.bfloat16).T
 
 
 VMEM = pl.BlockSpec(memory_space=pltpu.VMEM)
 LIMIT = pltpu.CompilerParams(vmem_limit_bytes=24 * 2**20)
+SPREAD_OUT = pltpu.CompilerParams(vmem_limit_bytes=24 * 2**20)
 
 
 def run(shift, q, kvs, state=None, n_out=1, head_at=0):
@@ -175,7 +180,7 @@
             bytes_accessed=4 * keys * HEAD_DIM + 2 * rows * heads * HEAD_DIM,
             transcendentals=rows * heads * keys,
         ),
-        compiler_params=LIMIT,
+        compiler_params=SPREAD_OUT,
     )(q, *kvs, *(() if first else (state,)))
 
 

time: 60.7 us -> 59.8 us (0.985)
  the two profiles are of different devices: /device:TPU:241 before, /device:TPU:305 now
where the time goes in v5:
time: 59.8 us; the launch traced here: 59.4 us
  starting transfers between devices  30.4 us (51%)
  waiting for transfers between devices  14.7 us (25%)
  Pallas kernels  14.1 us (24%)
    ppermute x5, starting transfers between devices, move(): return lax.ppermute(a, ('ctx', 'tp'), pairs)  18.9 us
    pallas_call x5, Pallas kernels, run(): pl.pallas_call(functools.partial(kernel, shift, len(kvs), head_at, heads,...  11.6 us
    all_to_all x1, waiting for transfers between devices, shards(): lax.all_to_all(spread(keys, values), 'ctx', 0, 0, axis_index_groups=groups)  10.7 us
    all_to_all x1, starting transfers between devices, shards(): lax.all_to_all(spread(keys, values), 'ctx', 0, 0, axis_index_groups=groups)  6.43 us
    ppermute x2, starting transfers between devices, swap(): return lax.ppermute(a, 'tp', [(i, i ^ 1) for i in range(Z * C)])  5.05 us
    ppermute x5, waiting for transfers between devices, move(): return lax.ppermute(a, ('ctx', 'tp'), pairs)  3.59 us
    pallas_call x1, Pallas kernels, spread(): pl.pallas_call(spread_kernel, in_specs=[hbm, hbm], out_specs=hbm, out_sha...  1.69 us
  transfers between devices with their start and end apart: 8, of which 3 were waited for; matrix products, arithmetic and copies ran while one was open for 0% of the time, Pallas kernels for 16%

profile of v5, /device:TPU:305, one launch (start us, length us, event | category | flops | bytes accessed | tf_op | source)
XLA Modules:
  0.0 59.4 jit_solution(4809693634369398416)
XLA Ops:
  0.0 0.0 copy-start
  0.0 1.7 %spread.1 = bf16[8,128,256]{2,1,0:T(8,128)(2,1)} custom-call(bf16[256,1024]{1,0:T(8,128)(2,1)} %keys_ref.1, bf16[256,1024]{1,0:T(8,128)(2,1)} %values_ref.1), custom_call_target="tpu_custom_call" | custom-call | tf_op jit(solution)/shard_map/spread/pallas_call | solution.py:212
  1.7 6.4 %all-to-all-start = ((bf16[8,128,256]{2,1,0:T(8,128)(2,1)}), bf16[8,128,256]{2,1,0:T(8,128)(2,1)S(1)}, u32[]{:S(2)}, u32[]{:S(2)}) async-start(bf16[8,128,256]{2,1,0:T(8,128)(2,1)} %spread.1), calls=%async_computation | async-start | bytes 1048576 | tf_op jit(solution)/shard_map/all_to_all | solution.py:242
  8.1 0.0 copy-done
  8.1 3.1 %collective-permute-start = (bf16[256,512]{1,0:T(8,128)(2,1)S(1)}, bf16[256,512]{1,0:T(8,128)(2,1)S(1)}, u32[]{:S(2)}, u32[]{:S(2)}) collective-permute-start(bf16[256,512]{1,0:T(8,128)(2,1)S(1)} %copy-done), channel_id=1, source_target_pairs={{0,1},{1,0},{2,3},{3,2},{4,5},{5,4},{6,7},{7,6},{8,9},{9,8},{10,11... | collective-permute-start | bytes 786440 | tf_op jit(solution)/shard_map/ppermute | solution.py:38
  11.3 10.7 %all-to-all-done = bf16[8,128,256]{2,1,0:T(8,128)(2,1)S(1)} async-done(((bf16[8,128,256]{2,1,0:T(8,128)(2,1)}), bf16[8,128,256]{2,1,0:T(8,128)(2,1)S(1)}, u32[]{:S(2)}, u32[]{:S(2)}) %all-to-all-start) | async-done | bytes 524320 | tf_op jit(solution)/shard_map/all_to_all | solution.py:242
  22.0 3.1 %collective-permute-start.5 = (bf16[1024,256]{1,0:T(8,128)(2,1)S(1)}, bf16[1024,256]{1,0:T(8,128)(2,1)S(1)}, u32[]{:S(2)}, u32[]{:S(2)}) collective-permute-start(bf16[1024,256]{1,0:T(8,128)(2,1)S(1)} %bitcast.3), channel_id=1, source_target_pairs={{0,48},{1,17},{2,50},{3,19},{4,52},{5,21},{6,54},{7,23},{8,56},{9,... | collective-permute-start | bytes 1572872 | tf_op jit(solution)/shard_map/ppermute | solution.py:34
  25.1 3.4 %collective-permute-start.1 = (bf16[512,256]{1,0:T(8,128)(2,1)S(1)}, bf16[512,256]{1,0:T(8,128)(2,1)S(1)}, u32[]{:S(2)}, u32[]{:S(2)}) collective-permute-start(bf16[512,256]{1,0:T(8,128)(2,1)S(1)} %bitcast.6), channel_id=1, source_target_pairs={{0,16},{1,49},{2,18},{3,51},{4,20},{5,53},{6,22},{7,55},{8,24},{9,... | collective-permute-start | bytes 786440 | tf_op jit(solution)/shard_map/ppermute | solution.py:34
  28.5 3.2 %collective-permute-start.3 = (bf16[512,256]{1,0:T(8,128)(2,1)S(1)}, bf16[512,256]{1,0:T(8,128)(2,1)S(1)}, u32[]{:S(2)}, u32[]{:S(2)}) collective-permute-start(bf16[512,256]{1,0:T(8,128)(2,1)S(1)} %bitcast.5), channel_id=1, source_target_pairs={{256,272},{257,305},{258,274},{259,307},{260,276},{261,309},{262,2... | collective-permute-start | bytes 786440 | tf_op jit(solution)/shard_map/ppermute | solution.py:34
  31.7 0.0 collective-permute-done
  31.8 3.6 %collective-permute-done.1.refs_1_ = bf16[512,256]{1,0:T(8,128)(2,1)S(1)} collective-permute-done((bf16[512,256]{1,0:T(8,128)(2,1)S(1)}, bf16[512,256]{1,0:T(8,128)(2,1)S(1)}, u32[]{:S(2)}, u32[]{:S(2)}) %collective-permute-start.1) | collective-permute-done | bytes 262176 | tf_op jit(solution)/shard_map/ppermute | solution.py:34
  35.3 4.6 %collective-permute-start.2 = (bf16[512,256]{1,0:T(8,128)(2,1)S(1)}, bf16[512,256]{1,0:T(8,128)(2,1)S(1)}, u32[]{:S(2)}, u32[]{:S(2)}) collective-permute-start(bf16[512,256]{1,0:T(8,128)(2,1)S(1)} %collective-permute-done.1.refs_1_), channel_id=1, source_target_pairs={{0,16},{1,49},{2,18},{3,51},{4,20},{5,53},{6,22},{7,55},{8,24},{9,... | collective-permute-start | bytes 786440 | tf_op jit(solution)/shard_map/ppermute | solution.py:34
  39.9 0.0 collective-permute-done.3.refs_2_
  39.9 4.7 %collective-permute-start.4 = (bf16[512,256]{1,0:T(8,128)(2,1)S(1)}, bf16[512,256]{1,0:T(8,128)(2,1)S(1)}, u32[]{:S(2)}, u32[]{:S(2)}) collective-permute-start(bf16[512,256]{1,0:T(8,128)(2,1)S(1)} %collective-permute-done.3.refs_2_), channel_id=1, source_target_pairs={{256,272},{257,305},{258,274},{259,307},{260,276},{261,309},{262,2... | collective-permute-start | bytes 786440 | tf_op jit(solution)/shard_map/ppermute | solution.py:34
  44.6 2.9 %shard_map.37.refs_3_ = f32[8,144,256]{2,1,0:T(8,128)S(1)} custom-call(bf16[256,1024]{1,0:T(8,128)(2,1)S(1)} %constant_dynamic-update-slice_fusion.refs_0_, bf16[1024,256]{1,0:T(8,128)(2,1)S(1)} %bitcast.4), custom_call_target="tpu_custom_call" | custom-call | flops 1073741824 | bytes 1048576 | tf_op jit(solution)/shard_map/pallas_call | solution.py:167
  47.5 2.8 %shard_map.38.refs_2_ = f32[8,144,256]{2,1,0:T(8,128)S(1)} custom-call(bf16[256,1024]{1,0:T(8,128)(2,1)S(1)} %constant_dynamic-update-slice_fusion.refs_0_, bf16[512,256]{1,0:T(8,128)(2,1)S(1)} %collective-permute-done.1.refs_1_, bf16[512,256]{1,0:T(8,128)(2,1)S(1)} %collective-permute-done.3.refs_2_, ...), custom_call_target="tpu_custom_call", output_to_operand_aliasing={{}: (3, {})} | custom-call | flops 1073741824 | bytes 1048576 | tf_op jit(solution)/shard_map/pallas_call | solution.py:167
  50.3 0.0 collective-permute-done.5.refs_1_
  50.4 2.5 %shard_map.39 = (f32[4,144,256]{2,1,0:T(8,128)S(1)}, f32[4,144,256]{2,1,0:T(8,128)S(1)}) custom-call(bf16[256,1024]{1,0:T(8,128)(2,1)S(1)} %constant_dynamic-update-slice_fusion.refs_0_, bf16[1024,256]{1,0:T(8,128)(2,1)S(1)} %collective-permute-done.5.refs_1_, f32[8,144,256]{2,1,0:T(8,128)S(1)} %shard_map.38.refs_2_), custom_call_target="tpu_custom_call" | custom-call | flops 1073741824 | bytes 1048576 | tf_op jit(solution)/shard_map/pallas_call | solution.py:167
  52.9 0.0 collective-permute-done.2.refs_1_
  52.9 0.0 collective-permute-done.4.refs_2_
  52.9 1.8 %shard_map.41 = f32[4,144,256]{2,1,0:T(8,128)S(1)} custom-call(bf16[256,1024]{1,0:T(8,128)(2,1)S(1)} %constant_dynamic-update-slice_fusion.refs_0_, bf16[512,256]{1,0:T(8,128)(2,1)S(1)} %collective-permute-done.2.refs_1_, bf16[512,256]{1,0:T(8,128)(2,1)S(1)} %collective-permute-done.4.refs_2_, ...), custom_call_target="tpu_custom_call", output_to_operand_aliasing={{}: (3, {})} | custom-call | flops 536870912 | bytes 786432 | tf_op jit(solution)/shard_map/pallas_call | solution.py:167
  54.7 1.9 %collective-permute-start.6 = (f32[4,144,256]{2,1,0:T(8,128)S(1)}, f32[4,144,256]{2,1,0:T(8,128)S(1)}, u32[]{:S(2)}, u32[]{:S(2)}) collective-permute-start(f32[4,144,256]{2,1,0:T(8,128)S(1)} %shard_map.41), channel_id=1, source_target_pairs={{0,1},{1,0},{2,3},{3,2},{4,5},{5,4},{6,7},{7,6},{8,9},{9,8},{10,11... | collective-permute-start | bytes 1769480 | tf_op jit(solution)/shard_map/ppermute | solution.py:38
  56.6 1.5 %shard_map.40.mine_ref = f32[4,144,256]{2,1,0:T(8,128)S(1)} custom-call(bf16[256,1024]{1,0:T(8,128)(2,1)S(1)} %constant_dynamic-update-slice_fusion.refs_0_, bf16[512,256]{1,0:T(8,128)(2,1)S(1)} %collective-permute-done.2.refs_1_, bf16[512,256]{1,0:T(8,128)(2,1)S(1)} %collective-permute-done.4.refs_2_, ...), custom_call_target="tpu_custom_call", output_to_operand_aliasing={{}: (3, {})} | custom-call | flops 536870912 | bytes 786432 | tf_op jit(solution)/shard_map/pallas_call | solution.py:167
  58.2 0.4 collective-permute-done.6.theirs_ref
  58.6 0.9 %merge.1 = bf16[256,512]{1,0:T(8,128)(2,1)} custom-call(f32[4,144,256]{2,1,0:T(8,128)S(1)} %shard_map.40.mine_ref, f32[4,144,256]{2,1,0:T(8,128)S(1)} %collective-permute-done.6.theirs_ref), custom_call_target="tpu_custom_call" | custom-call | flops 1048576 | bytes 1048576 | tf_op jit(solution)/shard_map/merge/pallas_call | solution.py:229
  (3 shorter events, 0.1 us)
Async XLA Ops:
  0.0 8.1 %copy-start = (bf16[256,512]{1,0:T(8,128)(2,1)S(1)}, bf16[256,512]{1,0:T(8,128)(2,1)}, u32[]{:S(2)}) copy-start(bf16[256,512]{1,0:T(8,128)(2,1)} %param.3) | copy-start | bytes 786436
  1.7 20.3 %all-to-all-start = ((bf16[8,128,256]{2,1,0:T(8,128)(2,1)}), bf16[8,128,256]{2,1,0:T(8,128)(2,1)S(1)}, u32[]{:S(2)}, u32[]{:S(2)}) async-start(bf16[8,128,256]{2,1,0:T(8,128)(2,1)} %spread.1), calls=%async_computation | async-start | bytes 1048576 | tf_op jit(solution)/shard_map/all_to_all | solution.py:242
  8.1 23.6 %collective-permute-start = (bf16[256,512]{1,0:T(8,128)(2,1)S(1)}, bf16[256,512]{1,0:T(8,128)(2,1)S(1)}, u32[]{:S(2)}, u32[]{:S(2)}) collective-permute-start(bf16[256,512]{1,0:T(8,128)(2,1)S(1)} %copy-done), channel_id=1, source_target_pairs={{0,1},{1,0},{2,3},{3,2},{4,5},{5,4},{6,7},{7,6},{8,9},{9,8},{10,11... | collective-permute-start | bytes 786440 | tf_op jit(solution)/shard_map/ppermute | solution.py:38
  22.0 28.4 %collective-permute-start.5 = (bf16[1024,256]{1,0:T(8,128)(2,1)S(1)}, bf16[1024,256]{1,0:T(8,128)(2,1)S(1)}, u32[]{:S(2)}, u32[]{:S(2)}) collective-permute-start(bf16[1024,256]{1,0:T(8,128)(2,1)S(1)} %bitcast.3), channel_id=1, source_target_pairs={{0,48},{1,17},{2,50},{3,19},{4,52},{5,21},{6,54},{7,23},{8,56},{9,... | collective-permute-start | bytes 1572872 | tf_op jit(solution)/shard_map/ppermute | solution.py:34
  25.1 10.2 %collective-permute-start.1 = (bf16[512,256]{1,0:T(8,128)(2,1)S(1)}, bf16[512,256]{1,0:T(8,128)(2,1)S(1)}, u32[]{:S(2)}, u32[]{:S(2)}) collective-permute-start(bf16[512,256]{1,0:T(8,128)(2,1)S(1)} %bitcast.6), channel_id=1, source_target_pairs={{0,16},{1,49},{2,18},{3,51},{4,20},{5,53},{6,22},{7,55},{8,24},{9,... | collective-permute-start | bytes 786440 | tf_op jit(solution)/shard_map/ppermute | solution.py:34
  28.5 11.4 %collective-permute-start.3 = (bf16[512,256]{1,0:T(8,128)(2,1)S(1)}, bf16[512,256]{1,0:T(8,128)(2,1)S(1)}, u32[]{:S(2)}, u32[]{:S(2)}) collective-permute-start(bf16[512,256]{1,0:T(8,128)(2,1)S(1)} %bitcast.5), channel_id=1, source_target_pairs={{256,272},{257,305},{258,274},{259,307},{260,276},{261,309},{262,2... | collective-permute-start | bytes 786440 | tf_op jit(solution)/shard_map/ppermute | solution.py:34
  35.3 17.5 %collective-permute-start.2 = (bf16[512,256]{1,0:T(8,128)(2,1)S(1)}, bf16[512,256]{1,0:T(8,128)(2,1)S(1)}, u32[]{:S(2)}, u32[]{:S(2)}) collective-permute-start(bf16[512,256]{1,0:T(8,128)(2,1)S(1)} %collective-permute-done.1.refs_1_), channel_id=1, source_target_pairs={{0,16},{1,49},{2,18},{3,51},{4,20},{5,53},{6,22},{7,55},{8,24},{9,... | collective-permute-start | bytes 786440 | tf_op jit(solution)/shard_map/ppermute | solution.py:34
  39.9 13.0 %collective-permute-start.4 = (bf16[512,256]{1,0:T(8,128)(2,1)S(1)}, bf16[512,256]{1,0:T(8,128)(2,1)S(1)}, u32[]{:S(2)}, u32[]{:S(2)}) collective-permute-start(bf16[512,256]{1,0:T(8,128)(2,1)S(1)} %collective-permute-done.3.refs_2_), channel_id=1, source_target_pairs={{256,272},{257,305},{258,274},{259,307},{260,276},{261,309},{262,2... | collective-permute-start | bytes 786440 | tf_op jit(solution)/shard_map/ppermute | solution.py:34
  54.7 3.9 %collective-permute-start.6 = (f32[4,144,256]{2,1,0:T(8,128)S(1)}, f32[4,144,256]{2,1,0:T(8,128)S(1)}, u32[]{:S(2)}, u32[]{:S(2)}) collective-permute-start(f32[4,144,256]{2,1,0:T(8,128)S(1)} %shard_map.41), channel_id=1, source_target_pairs={{0,1},{1,0},{2,3},{3,2},{4,5},{5,4},{6,7},{7,6},{8,9},{9,8},{10,11... | collective-permute-start | bytes 1769480 | tf_op jit(solution)/shard_map/ppermute | solution.py:38
